TPU v7x, 32 devices: a whole 2x2x4 slice. The times are simulated.
32 devices in a mesh: dp: 4 (over z), ctx: 4 (over y, core), tp: 2 (over x).
Axes of the slice: x: 2, y: 2, z: 4, core: 2. Of those that a mesh axis runs over, the one named last changes fastest.
Arguments:
- queries: bfloat16 [4, 512, 4096], P('dp', 'ctx', 'tp'), may hold values from -8 to 8
- keys_text: bfloat16 [4, 512, 512], P('dp', 'ctx', 'tp'), may hold values from -8 to 8
- values_text: bfloat16 [4, 512, 512], P('dp', 'ctx', 'tp'), may hold values from -6 to 6
- patch_rows: bfloat16 [4, 4, 8, 2, 512], P('dp', 'ctx', None, None, 'tp'), may hold values from -6 to 6
- patch_owner: int32 [4, 4, 8, 1], P('dp', 'ctx'), may hold values from 0 to 3; in each aligned block of 8 rows (0 to 7, 8 to 15, ..., all dimensions but the last counted through in order) at most 4 rows name the same one
- patch_place: int32 [4, 4, 8], P('dp', 'ctx'), may hold values from 0 to 127
- value_head: bfloat16 [4096], P('tp'), may hold values from -0.75 to 0.75
Outputs:
- attention: bfloat16 [4, 512, 4096], P('dp', 'ctx', 'tp')
- value_out: float32 [4, 512], P('dp', 'ctx')
Inputs may be any that keep to these rules, and one draw needn't show every extreme that they name: `patch_owner`: among the rows of one vision shard at most 4 name the same sequence, and exactly 4 do in some shards. `patch_place`: rows that share an owner, a ctx index and a position are all added there.
All inputs are finite; a program needn't handle non-finite values.
Results may differ from a plain program's by a relative error of at most 0.0079.
Values may be sent and summed in bfloat16 or wider, within the bound.
A program may use at most 64 MiB of HBM per device.

v0:
```python
import functools
import math

import jax
import jax.numpy as jnp
from jax import lax
from jax.experimental import pallas as pl
from jax.experimental.pallas import tpu as pltpu
from jax.sharding import PartitionSpec as P

HD = 128
CAP = 4
SLOT_BYTES = 8 * 2**20
MESH = pl.DeviceIdType.MESH


def attend_block(
    carried, query_split, query_place, block_keys, block_values, key_place, score_scale
):
    running_max, denominator, numerator = carried
    scores = (
        jnp.einsum("tgrd,sgd->tgrs", query_split, block_keys, preferred_element_type=jnp.float32)
        * score_scale
    )
    allowed = (key_place[None, :] <= query_place[:, None])[:, None, None, :]
    scores = jnp.where(allowed, scores, -1e30)
    new_max = jnp.maximum(running_max, jnp.max(scores, axis=-1))
    weights = jnp.where(allowed, jnp.exp(scores - new_max[..., None]), 0.0)
    shrink = jnp.exp(running_max - new_max)
    denominator = denominator * shrink + jnp.sum(weights, axis=-1)
    numerator = numerator * shrink[..., None] + jnp.einsum(
        "tgrs,sgd->tgrd",
        weights.astype(jnp.bfloat16),
        block_values,
        preferred_element_type=jnp.float32,
    )
    return (new_max, denominator, numerator)


def unchanged(carried):
    return carried


def collective_body(queries, keys_text, values_text, patch_rows, patch_owner, patch_place, value_head):
    token_count = queries.shape[1]
    kv_width = keys_text.shape[2]
    groups = kv_width // HD
    head_count = queries.shape[2] // HD
    group_size = head_count // groups
    score_scale = HD ** (-0.5)
    dp_count = lax.axis_size("dp")
    slot_count = dp_count * CAP
    owner_seq = patch_owner[0, 0, :, 0]
    places = patch_place[0, 0]
    owner_hits = (owner_seq[:, None] == jnp.arange(dp_count, dtype=jnp.int32)[None, :]).astype(
        jnp.int32
    )
    before = jnp.cumsum(owner_hits, axis=0) - owner_hits
    slot_rank = jnp.sum(before * owner_hits, axis=1)
    target = owner_seq * CAP + slot_rank
    select = (jnp.arange(slot_count, dtype=jnp.int32)[:, None] == target[None, :]).astype(jnp.int32)
    row_data = patch_rows[0, 0].reshape(places.shape[0], 2 * kv_width)
    packed = jnp.dot(
        select.astype(jnp.bfloat16), row_data, preferred_element_type=jnp.float32
    ).astype(jnp.bfloat16)
    filled = jnp.sum(select, axis=1)
    slot_place = jnp.sum(select * places[None, :], axis=1) + (1 - filled) * token_count
    packed = packed.reshape(slot_count, 2, kv_width)
    arrived, arrived_place = (
        lax.all_to_all(packed, "dp", split_axis=0, concat_axis=0, tiled=True),
        lax.all_to_all(slot_place, "dp", split_axis=0, concat_axis=0, tiled=True),
    )
    landing = (jnp.arange(token_count, dtype=jnp.int32)[:, None] == arrived_place[None, :]).astype(
        jnp.bfloat16
    )
    arrivals = jnp.dot(
        landing, arrived.reshape(slot_count, 2 * kv_width), preferred_element_type=jnp.float32
    )
    merged_keys = (keys_text[0].astype(jnp.float32) + arrivals[:, :kv_width]).astype(jnp.bfloat16)
    merged_values = (values_text[0].astype(jnp.float32) + arrivals[:, kv_width:]).astype(
        jnp.bfloat16
    )
    query_split = queries[0].reshape(token_count, groups, group_size, HD)
    first_row = lax.axis_index("ctx") * token_count
    query_place = first_row + jnp.arange(token_count, dtype=jnp.int32)
    initial = (
        jnp.full((token_count, groups, group_size), -1e30, jnp.float32),
        jnp.zeros((token_count, groups, group_size), jnp.float32),
        jnp.zeros((token_count, groups, group_size, HD), jnp.float32),
    )
    carried = initial
    start_row = jnp.int32(0)
    piece_keys = lax.all_gather(merged_keys, "ctx", axis=0, tiled=True)
    piece_values = lax.all_gather(merged_values, "ctx", axis=0, tiled=True)
    piece_rows = piece_keys.shape[0]
    block_rows = min(512, piece_rows)
    for lower in range(0, piece_rows, block_rows):
        upper = min(lower + block_rows, piece_rows)
        block_keys = piece_keys[lower:upper].reshape(upper - lower, groups, HD)
        block_values = piece_values[lower:upper].reshape(upper - lower, groups, HD)
        key_place = start_row + lower + jnp.arange(upper - lower, dtype=jnp.int32)

        def update(state_in):
            return attend_block(
                state_in, query_split, query_place, block_keys, block_values, key_place, score_scale
            )

        carried = lax.cond(
            start_row + lower <= first_row + token_count - 1, update, unchanged, carried
        )
    running_max, denominator, numerator = carried
    attention = (
        (numerator / denominator[..., None])
        .reshape(token_count, head_count * HD)
        .astype(jnp.bfloat16)
    )
    partial_value = jnp.dot(attention, value_head, preferred_element_type=jnp.float32)
    value_out = lax.psum(partial_value, "tp")
    return (attention[None], value_out[None])


def fused_kernel(
    dp_count,
    ctx_count,
    tp_count,
    owner_hbm,
    place_hbm,
    rows_hbm,
    keys_hbm,
    values_hbm,
    probe_hbm,
    queries_hbm,
    out_ref,
    value_ref,
    queries,
    text,
    rows_in,
    spots_in,
    merged_keys,
    merged_values,
    probe_raw,
    probe,
    partial,
    partial_in,
    query_sem,
    local_sem,
    text_send,
    text_recv,
    relay_send,
    patch_send,
    patch_recv,
    value_send,
    value_recv,
):
    d, c, t = lax.axis_index("dp"), lax.axis_index("ctx"), lax.axis_index("tp")
    token_count, kv_width = keys_hbm.shape
    groups = kv_width // HD
    heads = queries.shape[1] // HD
    group_size = heads // groups
    paired = ctx_count % 2 == 0
    side = lax.rem(c, 2)
    partner = c + 1 - 2 * side

    barrier = pltpu.get_barrier_semaphore()
    for k in range(dp_count):
        for m in range(ctx_count):
            if k or m:
                pl.semaphore_signal(
                    barrier,
                    inc=1,
                    device_id=(lax.rem(d + k, dp_count), lax.rem(c + m, ctx_count), t),
                    device_id_type=MESH,
                )
    for k in range(1, tp_count):
        pl.semaphore_signal(
            barrier, inc=1, device_id=(d, c, lax.rem(t + k, tp_count)), device_id_type=MESH
        )

    loads = [
        pltpu.make_async_copy(src, dst, local_sem.at[number])
        for number, (src, dst) in enumerate(
            (
                (rows_hbm, rows_in.at[c, d]),
                (owner_hbm, spots_in.at[c, d, 0]),
                (place_hbm, spots_in.at[c, d, 1]),
                (keys_hbm, text.at[c, 0]),
                (values_hbm, text.at[c, 1]),
                (probe_hbm, probe_raw),
            )
        )
    ]
    load_queries = pltpu.make_async_copy(queries_hbm, queries, query_sem)
    for load in loads:
        load.start()
    load_queries.start()
    for load in loads:
        load.wait()
    probe[...] = probe_raw[...].astype(jnp.float32)
    pl.semaphore_wait(barrier, dp_count * ctx_count - 1 + tp_count - 1)

    def patch_copies(k, later):
        there = lax.rem(d + k, dp_count)
        return [
            pltpu.make_async_remote_copy(
                src_ref=part.at[c, d],
                dst_ref=part.at[c, d],
                send_sem=patch_send.at[later, k, kind],
                recv_sem=patch_recv.at[c, d, kind],
                device_id=(there, later, t),
                device_id_type=MESH,
            )
            for kind, part in enumerate((rows_in, spots_in))
        ]

    def text_copies(later):
        return [
            pltpu.make_async_remote_copy(
                src_ref=text.at[c, kind],
                dst_ref=text.at[c, kind],
                send_sem=text_send.at[later, kind],
                recv_sem=text_recv.at[c, kind],
                device_id=(d, later, t),
                device_id_type=MESH,
            )
            for kind in range(2)
        ]

    def relay_copies(block):
        return [
            pltpu.make_async_remote_copy(
                src_ref=text.at[block, kind],
                dst_ref=text.at[block, kind],
                send_sem=relay_send.at[block, kind],
                recv_sem=text_recv.at[block, kind],
                device_id=(d, partner, t),
                device_id_type=MESH,
            )
            for kind in range(2)
        ]

    def sends_text(later):
        if not paired:
            return c < later
        return (c < later) & ((side == later % 2) | (partner == later))

    def for_patches(act):
        for k in range(dp_count):
            for later in range(ctx_count):
                reached = (c < later) if k == 0 else (c <= later)

                @pl.when(reached)
                def _():
                    for copy in patch_copies(k, later):
                        act(copy)

    def for_text(act):
        for later in range(1, ctx_count):

            @pl.when(sends_text(later))
            def _():
                for copy in text_copies(later):
                    act(copy)

    for_patches(lambda copy: copy.start())
    for_text(lambda copy: copy.start())

    def wait_text(block):
        for copy in relay_copies(block):
            copy.wait_recv()

    def wait_patches(block, first):
        for k in range(first, dp_count):
            there = lax.rem(d + k, dp_count)
            for kind, part in enumerate((rows_in, spots_in)):
                pltpu.make_async_remote_copy(
                    src_ref=part.at[block, there],
                    dst_ref=part.at[block, there],
                    send_sem=patch_send.at[0, k, kind],
                    recv_sem=patch_recv.at[block, there, kind],
                    device_id=(there, c, t),
                    device_id_type=MESH,
                ).wait_recv()

    def merge(block):
        slots = dp_count * rows_hbm.shape[0]
        spots = spots_in[block]
        code = spots[:, 0] * token_count + spots[:, 1]
        code = jnp.concatenate([code[k] for k in range(dp_count)], axis=1)
        here = d * token_count + lax.broadcasted_iota(jnp.int32, (token_count, slots), 0)
        landing = jnp.where(code == here, 1.0, 0.0).astype(jnp.bfloat16)
        rows = rows_in[block].astype(jnp.float32)
        row_keys = rows[:, :, 0, :].reshape(slots, kv_width).astype(jnp.bfloat16)
        row_values = rows[:, :, 1, :].reshape(slots, kv_width).astype(jnp.bfloat16)
        span = pl.ds(block * token_count, token_count)
        for kind, (rows, merged) in enumerate(
            ((row_keys, merged_keys), (row_values, merged_values))
        ):
            arrivals = jnp.dot(landing, rows, preferred_element_type=jnp.float32)
            merged[span, :] = (text[block, kind].astype(jnp.float32) + arrivals).astype(
                jnp.bfloat16
            )

    if paired:
        for block in range(ctx_count - 2):

            @pl.when((block < c) & (side == block % 2))
            def _():
                wait_text(block)

                @pl.when(block < c - side)
                def _():
                    for copy in relay_copies(block):
                        copy.start()

    for block in range(ctx_count):

        @pl.when(block == c)
        def _():
            wait_patches(block, 1)
            merge(block)

        @pl.when(block < c)
        def _():
            wait_patches(block, 0)
            if paired:

                @pl.when(side != block % 2)
                def _():
                    wait_text(block)

            else:
                wait_text(block)
            merge(block)

    load_queries.wait()
    score_scale = HD ** (-0.5) * math.log2(math.e)

    def attend(last):
        length = (last + 1) * token_count
        row = lax.broadcasted_iota(jnp.int32, (token_count, token_count), 0)
        col = lax.broadcasted_iota(jnp.int32, (token_count, token_count), 1)
        allowed = col <= row
        unroll = math.gcd(group_size, 4)

        def step(number, total):
            first = number * unroll
            lane = pl.multiple_of((first // group_size) * HD, HD)
            block_keys = merged_keys[0:length, pl.ds(lane, HD)]
            block_values = merged_values[0:length, pl.ds(lane, HD)]
            for extra in range(unroll):
                head = first + extra
                place = pl.ds(pl.multiple_of(head * HD, HD), HD)
                scores = lax.dot_general(
                    queries[:, place],
                    block_keys,
                    (((1,), (1,)), ((), ())),
                    preferred_element_type=jnp.float32,
                )
                parts = [
                    scores[:, j * token_count : (j + 1) * token_count] for j in range(last + 1)
                ]
                parts[last] = jnp.where(allowed, parts[last], -1e30)
                top = functools.reduce(jnp.maximum, parts)
                top = jnp.max(top, axis=1, keepdims=True)
                weights = [jnp.exp2((part - top) * score_scale) for part in parts]
                denominator = jnp.sum(
                    functools.reduce(jnp.add, weights), axis=1, keepdims=True
                )
                rounded = jnp.concatenate([w.astype(jnp.bfloat16) for w in weights], axis=1)
                numerator = jnp.dot(rounded, block_values, preferred_element_type=jnp.float32)
                result = (numerator * (1.0 / denominator)).astype(jnp.bfloat16)
                out_ref[:, place] = result
                total = total + result.astype(jnp.float32) * probe[pl.ds(head, 1), :]
            return total

        total = lax.fori_loop(
            0, heads // unroll, step, jnp.zeros((token_count, HD), jnp.float32)
        )
        partial[...] = jnp.sum(jnp.transpose(total), axis=0, keepdims=True)

    for last in range(ctx_count):

        @pl.when(c == last)
        def _():
            attend(last)

    value_copies = [
        pltpu.make_async_remote_copy(
            src_ref=partial,
            dst_ref=partial_in.at[k - 1],
            send_sem=value_send.at[k - 1],
            recv_sem=value_recv.at[k - 1],
            device_id=(d, c, lax.rem(t + k, tp_count)),
            device_id_type=MESH,
        )
        for k in range(1, tp_count)
    ]
    for copy in value_copies:
        copy.start()
    for_patches(lambda copy: copy.wait_send())
    for_text(lambda copy: copy.wait_send())
    if paired:
        for block in range(ctx_count - 2):

            @pl.when((block < c - side) & (side == block % 2))
            def _():
                for copy in relay_copies(block):
                    copy.wait_send()

    for copy in value_copies:
        copy.wait()
    whole = partial[...]
    for k in range(1, tp_count):
        whole = whole + partial_in[k - 1]
    value_ref[...] = whole


def fused_body(sizes, queries, keys_text, values_text, patch_rows, patch_owner, patch_place, value_head):
    dp_count, ctx_count, tp_count = sizes
    _, token_count, query_width = queries.shape
    kv_width = keys_text.shape[2]
    row_count = patch_rows.shape[2]
    heads = query_width // HD
    dma = pltpu.SemaphoreType.DMA
    vmem = pl.BlockSpec(memory_space=pltpu.VMEM)
    attention, value_out = pl.pallas_call(
        functools.partial(fused_kernel, dp_count, ctx_count, tp_count),
        out_shape=(
            jax.ShapeDtypeStruct((token_count, query_width), jnp.bfloat16),
            jax.ShapeDtypeStruct((1, token_count), jnp.float32),
        ),
        in_specs=[pl.BlockSpec(memory_space=pltpu.HBM)] * 7,
        out_specs=(vmem, vmem),
        scratch_shapes=[
            pltpu.VMEM((token_count, query_width), jnp.bfloat16),
            pltpu.VMEM((ctx_count, 2, token_count, kv_width), jnp.bfloat16),
            pltpu.VMEM((ctx_count, dp_count, row_count, 2, kv_width), jnp.bfloat16),
            pltpu.VMEM((ctx_count, dp_count, 2, 1, row_count), jnp.int32),
            pltpu.VMEM((ctx_count * token_count, kv_width), jnp.bfloat16),
            pltpu.VMEM((ctx_count * token_count, kv_width), jnp.bfloat16),
            pltpu.VMEM((heads, HD), jnp.bfloat16),
            pltpu.VMEM((heads, HD), jnp.float32),
            pltpu.VMEM((1, token_count), jnp.float32),
            pltpu.VMEM((max(tp_count - 1, 1), 1, token_count), jnp.float32),
            dma,
            dma((6,)),
            dma((ctx_count, 2)),
            dma((ctx_count, 2)),
            dma((ctx_count, 2)),
            dma((ctx_count, dp_count, 2)),
            dma((ctx_count, dp_count, 2)),
            dma((max(tp_count - 1, 1),)),
            dma((max(tp_count - 1, 1),)),
        ],
        compiler_params=pltpu.CompilerParams(
            collective_id=0, has_side_effects=True, vmem_limit_bytes=67043328
        ),
        name="merged_attention",
    )(
        patch_owner[0, 0].reshape(1, row_count),
        patch_place[0],
        patch_rows[0, 0],
        keys_text[0],
        values_text[0],
        value_head.reshape(heads, HD),
        queries[0],
    )
    return (attention[None], value_out)


def body(sizes, queries, keys_text, values_text, patch_rows, patch_owner, patch_place, value_head):
    dp_count, ctx_count, _ = sizes
    arriving = dp_count * ctx_count * patch_rows.size * patch_rows.dtype.itemsize
    arrays = (queries, keys_text, values_text, patch_rows, patch_owner, patch_place, value_head)
    if arriving > SLOT_BYTES:
        return collective_body(*arrays)
    return fused_body(sizes, *arrays)


def solution(mesh):
    in_specs = (
        P("dp", "ctx", "tp"),
        P("dp", "ctx", "tp"),
        P("dp", "ctx", "tp"),
        P("dp", "ctx", None, None, "tp"),
        P("dp", "ctx", None, None),
        P("dp", "ctx", None),
        P("tp"),
    )
    out_specs = (P("dp", "ctx", "tp"), P("dp", "ctx"))
    sizes = tuple(mesh.shape[axis] for axis in ("dp", "ctx", "tp"))
    return jax.shard_map(
        functools.partial(body, sizes),
        mesh=mesh,
        in_specs=in_specs,
        out_specs=out_specs,
        check_vma=False,
    )
```

profile of v0, /device:TPU:5, one launch (start us, length us, event | category | flops | bytes accessed | tf_op | source)
XLA Modules:
  0.0 24.9 jit_solution(10578577328938108616)
XLA Ops:
  0.6 21.9 %merged_attention.1 = (bf16[128,2048]{1,0:T(8,128)(2,1)}, f32[1,128]{1,0:T(1,128)}) custom-call(s32[1,8]{1,0:T(1,128)} %bitcast.14, s32[1,8]{1,0:T(1,128)} %bitcast.15, bf16[8,2,256]{2,1,0:T(2,128)(2,1)} %bitcast.12, bf16[128,256]{1,0:T(8,128)(2,1)} %bitcast.10, bf16[128,256]{1,0:T(8,128)(2,1)} %bitcast.11, bf16[16,128]{1,0:T(8,128)(2,1)} %bitcast.13, ...), custom_call_target="tpu_custom_call" | custom-call | tf_op jit(solution)/shard_map/merged_attention/pallas_call | solution.py:426
  22.5 0.0 copy-start
  22.5 1.9 %copy.11 = bf16[1,128,2048]{2,1,0:T(8,128)(2,1)} copy(bf16[1,128,2048]{2,1,0:T(8,128)(2,1)} %bitcast.9) | data formatting | bytes 1048576
  24.4 0.0 copy-done
  24.4 0.5 %copy.12 = f32[1,128]{1,0:T(1,128)} copy(f32[1,128]{1,0:T(1,128)S(1)} %copy-done) | data formatting | bytes 1024
Async XLA Ops:
  22.5 1.9 %copy-start = (f32[1,128]{1,0:T(1,128)S(1)}, f32[1,128]{1,0:T(1,128)}, u32[]{:S(2)}) copy-start(f32[1,128]{1,0:T(1,128)} %get-tuple-element.9) | copy-start | bytes 1540
where the time goes:
time: 25.1 us; the launch traced here: 24.9 us
  Pallas kernels  21.9 us (87%)
  local copies, waits for them, and re-layouts  2.4 us (10%)
  between operations  0.65 us (3%)
    pallas_call x1, Pallas kernels, fused_body(): pl.pallas_call(functools.partial(fused_kernel, dp_count, ctx_count, tp_co...  21.9 us
    unnamed x4, local copies, waits for them, and re-layouts  2.4 us

commit v1 on v0

v1 whole, which is shorter than its diff:
```python
import functools
import math

import jax
import jax.numpy as jnp
from jax import lax
from jax.experimental import pallas as pl
from jax.experimental.pallas import tpu as pltpu
from jax.sharding import PartitionSpec as P

HD = 128
CAP = 4
SLOT_BYTES = 8 * 2**20
MESH = pl.DeviceIdType.MESH


def attend_block(
    carried, query_split, query_place, block_keys, block_values, key_place, score_scale
):
    running_max, denominator, numerator = carried
    scores = (
        jnp.einsum("tgrd,sgd->tgrs", query_split, block_keys, preferred_element_type=jnp.float32)
        * score_scale
    )
    allowed = (key_place[None, :] <= query_place[:, None])[:, None, None, :]
    scores = jnp.where(allowed, scores, -1e30)
    new_max = jnp.maximum(running_max, jnp.max(scores, axis=-1))
    weights = jnp.where(allowed, jnp.exp(scores - new_max[..., None]), 0.0)
    shrink = jnp.exp(running_max - new_max)
    denominator = denominator * shrink + jnp.sum(weights, axis=-1)
    numerator = numerator * shrink[..., None] + jnp.einsum(
        "tgrs,sgd->tgrd",
        weights.astype(jnp.bfloat16),
        block_values,
        preferred_element_type=jnp.float32,
    )
    return (new_max, denominator, numerator)


def unchanged(carried):
    return carried


def collective_body(queries, keys_text, values_text, patch_rows, patch_owner, patch_place, value_head):
    token_count = queries.shape[1]
    kv_width = keys_text.shape[2]
    groups = kv_width // HD
    head_count = queries.shape[2] // HD
    group_size = head_count // groups
    score_scale = HD ** (-0.5)
    dp_count = lax.axis_size("dp")
    slot_count = dp_count * CAP
    owner_seq = patch_owner[0, 0, :, 0]
    places = patch_place[0, 0]
    owner_hits = (owner_seq[:, None] == jnp.arange(dp_count, dtype=jnp.int32)[None, :]).astype(
        jnp.int32
    )
    before = jnp.cumsum(owner_hits, axis=0) - owner_hits
    slot_rank = jnp.sum(before * owner_hits, axis=1)
    target = owner_seq * CAP + slot_rank
    select = (jnp.arange(slot_count, dtype=jnp.int32)[:, None] == target[None, :]).astype(jnp.int32)
    row_data = patch_rows[0, 0].reshape(places.shape[0], 2 * kv_width)
    packed = jnp.dot(
        select.astype(jnp.bfloat16), row_data, preferred_element_type=jnp.float32
    ).astype(jnp.bfloat16)
    filled = jnp.sum(select, axis=1)
    slot_place = jnp.sum(select * places[None, :], axis=1) + (1 - filled) * token_count
    packed = packed.reshape(slot_count, 2, kv_width)
    arrived, arrived_place = (
        lax.all_to_all(packed, "dp", split_axis=0, concat_axis=0, tiled=True),
        lax.all_to_all(slot_place, "dp", split_axis=0, concat_axis=0, tiled=True),
    )
    landing = (jnp.arange(token_count, dtype=jnp.int32)[:, None] == arrived_place[None, :]).astype(
        jnp.bfloat16
    )
    arrivals = jnp.dot(
        landing, arrived.reshape(slot_count, 2 * kv_width), preferred_element_type=jnp.float32
    )
    merged_keys = (keys_text[0].astype(jnp.float32) + arrivals[:, :kv_width]).astype(jnp.bfloat16)
    merged_values = (values_text[0].astype(jnp.float32) + arrivals[:, kv_width:]).astype(
        jnp.bfloat16
    )
    query_split = queries[0].reshape(token_count, groups, group_size, HD)
    first_row = lax.axis_index("ctx") * token_count
    query_place = first_row + jnp.arange(token_count, dtype=jnp.int32)
    initial = (
        jnp.full((token_count, groups, group_size), -1e30, jnp.float32),
        jnp.zeros((token_count, groups, group_size), jnp.float32),
        jnp.zeros((token_count, groups, group_size, HD), jnp.float32),
    )
    carried = initial
    start_row = jnp.int32(0)
    piece_keys = lax.all_gather(merged_keys, "ctx", axis=0, tiled=True)
    piece_values = lax.all_gather(merged_values, "ctx", axis=0, tiled=True)
    piece_rows = piece_keys.shape[0]
    block_rows = min(512, piece_rows)
    for lower in range(0, piece_rows, block_rows):
        upper = min(lower + block_rows, piece_rows)
        block_keys = piece_keys[lower:upper].reshape(upper - lower, groups, HD)
        block_values = piece_values[lower:upper].reshape(upper - lower, groups, HD)
        key_place = start_row + lower + jnp.arange(upper - lower, dtype=jnp.int32)

        def update(state_in):
            return attend_block(
                state_in, query_split, query_place, block_keys, block_values, key_place, score_scale
            )

        carried = lax.cond(
            start_row + lower <= first_row + token_count - 1, update, unchanged, carried
        )
    running_max, denominator, numerator = carried
    attention = (
        (numerator / denominator[..., None])
        .reshape(token_count, head_count * HD)
        .astype(jnp.bfloat16)
    )
    partial_value = jnp.dot(attention, value_head, preferred_element_type=jnp.float32)
    value_out = lax.psum(partial_value, "tp")
    return (attention[None], value_out[None])


def attend_rows(queries, merged_keys, merged_values, probe, out, heads, group, last, token_count):
    group_size = heads // merged_keys.shape[0]
    first = group * group_size
    length = (last + 1) * token_count
    rows = math.gcd(token_count, 32)
    score_scale = HD ** (-0.5) * math.log2(math.e)
    block_keys = merged_keys[group, 0:length, :]
    block_values = merged_values[group, 0:length, :]
    places = [
        pl.ds(pl.multiple_of((first + extra) * HD, HD), HD) for extra in range(group_size)
    ]
    totals = []
    for lower in range(0, token_count, rows):
        span = slice(lower, lower + rows)
        stacked = jnp.concatenate([queries[span, place] for place in places], axis=0)
        scores = lax.dot_general(
            stacked, block_keys, (((1,), (1,)), ((), ())), preferred_element_type=jnp.float32
        )
        row = lower + lax.broadcasted_iota(jnp.int32, (rows, token_count), 0)
        col = lax.broadcasted_iota(jnp.int32, (rows, token_count), 1)
        allowed = jnp.concatenate([col <= row] * group_size, axis=0)
        parts = [scores[:, j * token_count : (j + 1) * token_count] for j in range(last + 1)]
        parts[last] = jnp.where(allowed, parts[last], -1e30)
        top = jnp.max(functools.reduce(jnp.maximum, parts), axis=1, keepdims=True)
        weights = [jnp.exp2((part - top) * score_scale) for part in parts]
        rounded = jnp.concatenate([w.astype(jnp.bfloat16) for w in weights], axis=1)
        sums = jnp.dot(rounded, block_values, preferred_element_type=jnp.float32)
        result = (sums[:, :HD] * (1.0 / sums[:, HD:])).astype(jnp.bfloat16)
        total = jnp.zeros((rows, HD), jnp.float32)
        for extra in range(group_size):
            piece = result[extra * rows : (extra + 1) * rows]
            out[span, places[extra]] = piece
            total = total + piece.astype(jnp.float32) * probe[pl.ds(first + extra, 1), :]
        totals.append(total)
    return jnp.concatenate(totals, axis=0)


def fused_kernel(
    sizes,
    owner_hbm,
    place_hbm,
    rows_hbm,
    keys_hbm,
    values_hbm,
    probe_hbm,
    queries_hbm,
    out_any,
    value_ref,
    queries,
    out,
    text,
    rows_in,
    spots_in,
    merged_keys,
    merged_values,
    probe_raw,
    probe,
    partial,
    partial_in,
    query_sem,
    out_sem,
    local_sem,
    text_send,
    text_recv,
    relay_send,
    patch_send,
    patch_recv,
    pass_send,
    pass_recv,
    value_send,
    value_recv,
):
    dp_count, ctx_count, tp_count = sizes
    d, c, t = lax.axis_index("dp"), lax.axis_index("ctx"), lax.axis_index("tp")
    token_count, kv_width = keys_hbm.shape
    groups = kv_width // HD
    heads = queries.shape[1] // HD
    chips = ctx_count // 2
    side = lax.rem(c, 2)
    chip = c // 2
    partner = c + 1 - 2 * side

    barrier = pltpu.get_barrier_semaphore()

    def greet(device):
        pl.semaphore_signal(barrier, inc=1, device_id=device, device_id_type=MESH)

    greet((d, partner, t))
    for k in range(dp_count):
        for m in range(chips):
            if k or m:
                greet((lax.rem(d + k, dp_count), lax.rem(c + 2 * m, ctx_count), t))
    for k in range(1, tp_count):
        greet((d, c, lax.rem(t + k, tp_count)))
    greetings = dp_count * chips + tp_count - 1

    def lanes(group):
        return slice(group * HD, (group + 1) * HD)

    sources = [
        (rows_hbm, rows_in.at[c, d]),
        (owner_hbm, spots_in.at[c, d, 0]),
        (place_hbm, spots_in.at[c, d, 1]),
        (probe_hbm, probe_raw),
    ]
    for group in range(groups):
        sources.append((keys_hbm.at[:, lanes(group)], text.at[c, group, 0]))
        sources.append((values_hbm.at[:, lanes(group)], text.at[c, group, 1]))
    loads = [
        pltpu.make_async_copy(src, dst, local_sem.at[number])
        for number, (src, dst) in enumerate(sources)
    ]
    load_queries = pltpu.make_async_copy(queries_hbm, queries, query_sem)
    for load in loads:
        load.start()
    load_queries.start()
    merged_values[:, :, HD:] = jnp.ones(
        (groups, ctx_count * token_count, HD), jnp.bfloat16
    )
    with jax.named_scope("w_loads"):
        for load in loads:
            load.wait()
    probe[...] = probe_raw[...].astype(jnp.float32)
    with jax.named_scope("w_barrier"):
        pl.semaphore_wait(barrier, greetings)

    parts = (rows_in, spots_in)

    def patch_copies(k, m):
        there = lax.rem(d + k, dp_count)
        later = c if m == 0 else 2 * m + side
        return [
            pltpu.make_async_remote_copy(
                src_ref=part.at[c, d],
                dst_ref=part.at[c, d],
                send_sem=patch_send.at[k, m, kind],
                recv_sem=patch_recv.at[c, d, kind],
                device_id=(there, later, t),
                device_id_type=MESH,
            )
            for kind, part in enumerate(parts)
        ]

    def for_patches(act):
        for k in range(1, dp_count):
            for copy in patch_copies(k, 0):
                act(copy)
        for k in range(dp_count):
            for m in range(1, chips):

                @pl.when(chip < m)
                def _():
                    for copy in patch_copies(k, m):
                        act(copy)

    def pass_copies(block):
        return [
            pltpu.make_async_remote_copy(
                src_ref=part.at[block],
                dst_ref=part.at[block],
                send_sem=pass_send.at[block, kind],
                recv_sem=pass_recv.at[block, kind],
                device_id=(d, partner, t),
                device_id_type=MESH,
            )
            for kind, part in enumerate(parts)
        ]

    def text_copy(m, group):
        return pltpu.make_async_remote_copy(
            src_ref=text.at[c, group],
            dst_ref=text.at[c, group],
            send_sem=text_send.at[m, group],
            recv_sem=text_recv.at[c, group],
            device_id=(d, 2 * m + side, t),
            device_id_type=MESH,
        )

    def relay_copy(block, group):
        return pltpu.make_async_remote_copy(
            src_ref=text.at[block, group],
            dst_ref=text.at[block, group],
            send_sem=relay_send.at[block, group],
            recv_sem=text_recv.at[block, group],
            device_id=(d, partner, t),
            device_id_type=MESH,
        )

    def for_text(act):
        for group in range(groups):
            for m in range(1, chips):

                @pl.when(chip < m)
                def _():
                    act(text_copy(m, group))

    def relays(block):
        return (block < c + 1 - side) & (side == block % 2)

    with jax.named_scope("starts"):
        for_patches(lambda copy: copy.start())
        for_text(lambda copy: copy.start())

    def wait_patches(block):
        for k in range(1, dp_count):
            there = lax.rem(d + k, dp_count)
            for kind, part in enumerate(parts):
                pltpu.make_async_remote_copy(
                    src_ref=part.at[block, there],
                    dst_ref=part.at[block, there],
                    send_sem=patch_send.at[k, 0, kind],
                    recv_sem=patch_recv.at[block, there, kind],
                    device_id=(there, c, t),
                    device_id_type=MESH,
                ).wait_recv()

    def wait_own_patches(block):
        for kind, part in enumerate(parts):
            pltpu.make_async_remote_copy(
                src_ref=part.at[block, d],
                dst_ref=part.at[block, d],
                send_sem=patch_send.at[0, 0, kind],
                recv_sem=patch_recv.at[block, d, kind],
                device_id=(d, partner, t),
                device_id_type=MESH,
            ).wait_recv()

    def merge(block):
        slots = dp_count * rows_hbm.shape[0]
        spots = spots_in[block]
        code = spots[:, 0] * token_count + spots[:, 1]
        code = jnp.concatenate([code[k] for k in range(dp_count)], axis=1)
        here = d * token_count + lax.broadcasted_iota(jnp.int32, (token_count, slots), 0)
        landing = jnp.where(code == here, 1.0, 0.0).astype(jnp.bfloat16)
        rows = rows_in[block].astype(jnp.float32)
        span = pl.ds(block * token_count, token_count)
        for kind in range(2):
            kind_rows = rows[:, :, kind, :].reshape(slots, kv_width).astype(jnp.bfloat16)
            arrivals = jnp.dot(landing, kind_rows, preferred_element_type=jnp.float32)
            for group in range(groups):
                whole = text[block, group, kind].astype(jnp.float32) + arrivals[:, lanes(group)]
                if kind == 0:
                    merged_keys[group, span, :] = whole.astype(jnp.bfloat16)
                else:
                    merged_values[group, span, 0:HD] = whole.astype(jnp.bfloat16)

    with jax.named_scope("patches"):
        for block in range(ctx_count):

            @pl.when((block <= c) & (side == block % 2))
            def _():
                wait_patches(block)

                @pl.when(block < c)
                def _():
                    wait_own_patches(block)

                @pl.when(relays(block))
                def _():
                    for copy in pass_copies(block):
                        copy.start()

    with jax.named_scope("own"):

        @pl.when(side == 0)
        def _():
            for group in range(groups):
                relay_copy(c, group).start()

        for block in range(ctx_count):

            @pl.when(block == c)
            def _():
                merge(block)

    with jax.named_scope("relay"):
        for group in range(groups):
            for block in range(ctx_count - 2):

                @pl.when((block < c - side) & (side == block % 2))
                def _():
                    relay_copy(block, group).wait_recv()
                    relay_copy(block, group).start()

    with jax.named_scope("merges"):
        for block in range(ctx_count - 1):

            @pl.when((block < c) & (side != block % 2))
            def _():
                for copy in pass_copies(block):
                    copy.wait_recv()
                for group in range(groups):
                    relay_copy(block, group).wait_recv()
                merge(block)

            if block < ctx_count - 2:

                @pl.when((block < c) & (side == block % 2))
                def _():
                    merge(block)

    load_queries.wait()

    def out_copy(group):
        width = queries.shape[1] // groups
        place = pl.ds(pl.multiple_of(group * width, width), width)
        return pltpu.make_async_copy(out.at[:, place], out_any.at[:, place], out_sem.at[group])

    def attend(last):
        def step(group, total):
            total = total + attend_rows(
                queries, merged_keys, merged_values, probe, out, heads, group, last, token_count
            )
            out_copy(group).start()
            return total

        total = lax.fori_loop(0, groups, step, jnp.zeros((token_count, HD), jnp.float32))
        partial[...] = jnp.sum(jnp.transpose(total), axis=0, keepdims=True)

    with jax.named_scope("attend"):
        for last in range(ctx_count):

            @pl.when(c == last)
            def _():
                attend(last)

    value_copies = [
        pltpu.make_async_remote_copy(
            src_ref=partial,
            dst_ref=partial_in.at[k - 1],
            send_sem=value_send.at[k - 1],
            recv_sem=value_recv.at[k - 1],
            device_id=(d, c, lax.rem(t + k, tp_count)),
            device_id_type=MESH,
        )
        for k in range(1, tp_count)
    ]
    for copy in value_copies:
        copy.start()
    with jax.named_scope("tail"):
        for_patches(lambda copy: copy.wait_send())
        for_text(lambda copy: copy.wait_send())
        for block in range(ctx_count):

            @pl.when(relays(block))
            def _():
                for copy in pass_copies(block):
                    copy.wait_send()
                for group in range(groups):
                    relay_copy(block, group).wait_send()

        for group in range(groups):
            out_copy(group).wait()
        for copy in value_copies:
            copy.wait()
    whole = partial[...]
    for k in range(1, tp_count):
        whole = whole + partial_in[k - 1]
    value_ref[...] = whole


def write_kernel(attention, value, attention_hbm, value_hbm, sems):
    pieces = sems.shape[0] - 1
    rows = attention.shape[0] // pieces
    copies = [pltpu.make_async_copy(value, value_hbm, sems.at[pieces])]
    for number in range(pieces):
        span = pl.ds(number * rows, rows)
        copies.append(
            pltpu.make_async_copy(
                attention.at[span, :], attention_hbm.at[span, :], sems.at[number]
            )
        )
    for copy in copies:
        copy.start()
    for copy in copies:
        copy.wait()


def fused_body(sizes, queries, keys_text, values_text, patch_rows, patch_owner, patch_place, value_head):
    dp_count, ctx_count, tp_count = sizes
    _, token_count, query_width = queries.shape
    kv_width = keys_text.shape[2]
    row_count = patch_rows.shape[2]
    heads = query_width // HD
    groups = kv_width // HD
    dma = pltpu.SemaphoreType.DMA
    vmem = pl.BlockSpec(memory_space=pltpu.VMEM)
    anywhere = pl.BlockSpec(memory_space=pl.ANY)
    others = max(tp_count - 1, 1)
    inputs = (
        patch_owner[0, 0].reshape(1, row_count),
        patch_place[0],
        patch_rows[0, 0],
        keys_text[0],
        values_text[0],
        value_head.reshape(heads, HD),
        queries[0],
    )
    shapes = (
        jax.ShapeDtypeStruct((token_count, query_width), jnp.bfloat16),
        jax.ShapeDtypeStruct((1, token_count), jnp.float32),
    )
    attention, value_out = pl.pallas_call(
        functools.partial(fused_kernel, sizes),
        out_shape=shapes,
        in_specs=[pl.BlockSpec(memory_space=pltpu.HBM)] * 7,
        out_specs=(anywhere, vmem),
        scratch_shapes=[
            pltpu.VMEM((token_count, query_width), jnp.bfloat16),
            pltpu.VMEM((token_count, query_width), jnp.bfloat16),
            pltpu.VMEM((ctx_count, groups, 2, token_count, HD), jnp.bfloat16),
            pltpu.VMEM((ctx_count, dp_count, row_count, 2, kv_width), jnp.bfloat16),
            pltpu.VMEM((ctx_count, dp_count, 2, 1, row_count), jnp.int32),
            pltpu.VMEM((groups, ctx_count * token_count, HD), jnp.bfloat16),
            pltpu.VMEM((groups, ctx_count * token_count, 2 * HD), jnp.bfloat16),
            pltpu.VMEM((heads, HD), jnp.bfloat16),
            pltpu.VMEM((heads, HD), jnp.float32),
            pltpu.VMEM((1, token_count), jnp.float32),
            pltpu.VMEM((others, 1, token_count), jnp.float32),
            dma,
            dma((groups,)),
            dma((4 + 2 * groups,)),
            dma((ctx_count // 2, groups)),
            dma((ctx_count, groups)),
            dma((ctx_count, groups)),
            dma((dp_count, ctx_count // 2, 2)),
            dma((ctx_count, dp_count, 2)),
            dma((ctx_count, 2)),
            dma((ctx_count, 2)),
            dma((others,)),
            dma((others,)),
        ],
        compiler_params=pltpu.CompilerParams(
            collective_id=0, has_side_effects=True, vmem_limit_bytes=24 * 2**20
        ),
        name="merged_attention",
    )(*(pltpu.with_memory_space_constraint(array, pltpu.HBM) for array in inputs))
    attention, value_out = pl.pallas_call(
        write_kernel,
        out_shape=shapes,
        in_specs=[anywhere] * 2,
        out_specs=(pl.BlockSpec(memory_space=pltpu.HBM),) * 2,
        scratch_shapes=[dma((math.gcd(token_count // 16, 4) + 1,))],
        compiler_params=pltpu.CompilerParams(vmem_limit_bytes=2**20),
        name="write_out",
    )(*(pltpu.with_memory_space_constraint(array, pltpu.VMEM) for array in (attention, value_out)))
    return (attention[None], value_out)


def body(sizes, queries, keys_text, values_text, patch_rows, patch_owner, patch_place, value_head):
    dp_count, ctx_count, _ = sizes
    arriving = dp_count * ctx_count * patch_rows.size * patch_rows.dtype.itemsize
    arrays = (queries, keys_text, values_text, patch_rows, patch_owner, patch_place, value_head)
    if arriving > SLOT_BYTES or ctx_count % 2:
        return collective_body(*arrays)
    return fused_body(sizes, *arrays)


def solution(mesh):
    in_specs = (
        P("dp", "ctx", "tp"),
        P("dp", "ctx", "tp"),
        P("dp", "ctx", "tp"),
        P("dp", "ctx", None, None, "tp"),
        P("dp", "ctx", None, None),
        P("dp", "ctx", None),
        P("tp"),
    )
    out_specs = (P("dp", "ctx", "tp"), P("dp", "ctx"))
    sizes = tuple(mesh.shape[axis] for axis in ("dp", "ctx", "tp"))
    return jax.shard_map(
        functools.partial(body, sizes),
        mesh=mesh,
        in_specs=in_specs,
        out_specs=out_specs,
        check_vma=False,
    )
```

time: 25.1 us -> 18.2 us (0.73)
  Pallas kernels: 21.9 us -> 17.4 us
  local copies, waits for them, and re-layouts: 2.4 us -> 0 us
    pallas_call x1 -> x2, Pallas kernels: 21.9 us -> 17.4 us  [the longest x1 16.5 us: fused_body(): pl.pallas_call(functools.partial(fused_kernel, sizes), out_shape=shapes,...]
    unnamed x4 -> x0, local copies, waits for them, and re-layouts: 2.4 us -> none
where the time goes in v1:
time: 18.2 us; the launch traced here: 18 us
  Pallas kernels  17.4 us (96%)
  between operations  0.64 us (4%)
    pallas_call x1, Pallas kernels, fused_body(): pl.pallas_call(functools.partial(fused_kernel, sizes), out_shape=shapes,...  16.5 us
    pallas_call x1, Pallas kernels, fused_body(): pl.pallas_call(write_kernel, out_shape=shapes, in_specs=[anywhere] * 2, o...  0.83 us

profile of v1, /device:TPU:5, one launch (start us, length us, event | category | flops | bytes accessed | tf_op | source)
XLA Modules:
  0.0 18.0 jit_solution(13718353807941412024)
XLA Ops:
  0.6 16.5 %merged_attention.1 = (bf16[128,2048]{1,0:T(8,128)(2,1)S(1)}, f32[1,128]{1,0:T(1,128)S(1)}) custom-call(s32[1,8]{1,0:T(1,128)} %bitcast.13, s32[1,8]{1,0:T(1,128)} %bitcast.14, bf16[8,2,256]{2,1,0:T(2,128)(2,1)} %bitcast.11, bf16[128,256]{1,0:T(8,128)(2,1)} %bitcast.9, bf16[128,256]{1,0:T(8,128)(2,1)} %bitcast.10, bf16[16,128]{1,0:T(8,128)(2,1)} %bitcast.12, ...), custom_call_target="tpu_custom_call" | custom-call | tf_op jit(solution)/shard_map/merged_attention/pallas_call | solution.py:524
  17.2 0.8 %write_out.1 = (bf16[128,2048]{1,0:T(8,128)(2,1)}, f32[1,128]{1,0:T(1,128)}) custom-call(bf16[128,2048]{1,0:T(8,128)(2,1)S(1)} %get-tuple-element.6.attention, f32[1,128]{1,0:T(1,128)S(1)} %get-tuple-element.7.value), custom_call_target="tpu_custom_call" | custom-call | tf_op jit(solution)/shard_map/write_out/pallas_call | solution.py:559

commit v2 on v1

--- a/solution.py
+++ b/solution.py
@@ -186,248 +186,197 @@
     relay_send,
     patch_send,
     patch_recv,
-    pass_send,
-    pass_recv,
     value_send,
     value_recv,
+    ready,
 ):
     dp_count, ctx_count, tp_count = sizes
     d, c, t = lax.axis_index("dp"), lax.axis_index("ctx"), lax.axis_index("tp")
     token_count, kv_width = keys_hbm.shape
+    row_count = rows_hbm.shape[0]
     groups = kv_width // HD
     heads = queries.shape[1] // HD
     chips = ctx_count // 2
     side = lax.rem(c, 2)
     chip = c // 2
-    partner = c + 1 - 2 * side
 
     barrier = pltpu.get_barrier_semaphore()
 
     def greet(device):
         pl.semaphore_signal(barrier, inc=1, device_id=device, device_id_type=MESH)
 
-    greet((d, partner, t))
-    for k in range(dp_count):
-        for m in range(chips):
-            if k or m:
-                greet((lax.rem(d + k, dp_count), lax.rem(c + 2 * m, ctx_count), t))
+    for m in range(1, ctx_count):
+        greet((d, lax.rem(c + m, ctx_count), t))
     for k in range(1, tp_count):
         greet((d, c, lax.rem(t + k, tp_count)))
-    greetings = dp_count * chips + tp_count - 1
+
+    def greet_above(there, carry):
+        for block in range(ctx_count):
+            greet((there, block, t))
+        return carry
+
+    lax.fori_loop(d + 1, dp_count, greet_above, 0)
 
     def lanes(group):
         return slice(group * HD, (group + 1) * HD)
 
-    sources = [
-        (rows_hbm, rows_in.at[c, d]),
-        (owner_hbm, spots_in.at[c, d, 0]),
-        (place_hbm, spots_in.at[c, d, 1]),
-        (probe_hbm, probe_raw),
+    def copy_of(src, dst, sem):
+        return pltpu.make_async_copy(src, dst, sem)
+
+    def wait_bytes(ref, sem):
+        copy_of(ref, ref, sem).wait()
+
+    own = c * dp_count + d
+    load_patches = [
+        copy_of(rows_hbm, rows_in.at[own], local_sem.at[0]),
+        copy_of(owner_hbm, spots_in.at[own, 0], local_sem.at[1]),
+        copy_of(place_hbm, spots_in.at[own, 1], local_sem.at[1]),
     ]
+    load_probe = copy_of(probe_hbm, probe_raw, local_sem.at[2])
+    load_queries = copy_of(queries_hbm, queries, query_sem)
+    for load in load_patches:
+        load.start()
     for group in range(groups):
-        sources.append((keys_hbm.at[:, lanes(group)], text.at[c, group, 0]))
-        sources.append((values_hbm.at[:, lanes(group)], text.at[c, group, 1]))
-    loads = [
-        pltpu.make_async_copy(src, dst, local_sem.at[number])
-        for number, (src, dst) in enumerate(sources)
-    ]
-    load_queries = pltpu.make_async_copy(queries_hbm, queries, query_sem)
-    for load in loads:
-        load.start()
+        for kind, source in enumerate((keys_hbm, values_hbm)):
+            copy_of(
+                source.at[:, lanes(group)], text.at[c, group, kind], text_recv.at[c, group]
+            ).start()
+    load_probe.start()
     load_queries.start()
-    merged_values[:, :, HD:] = jnp.ones(
-        (groups, ctx_count * token_count, HD), jnp.bfloat16
-    )
+    merged_values[:, :, HD:] = jnp.ones((groups, ctx_count * token_count, HD), jnp.bfloat16)
+    with jax.named_scope("w_barrier"):
+        pl.semaphore_wait(barrier, ctx_count - 1 + tp_count - 1 + d * ctx_count)
+
+    def announce(there, carry):
+        def to_block(block, inner):
+            pl.semaphore_signal(
+                ready.at[d], inc=1, device_id=(there, block, t), device_id_type=MESH
+            )
+            return inner
+
+        return lax.fori_loop(0, c + 1, to_block, carry)
+
+    lax.fori_loop(0, d, announce, 0)
     with jax.named_scope("w_loads"):
-        for load in loads:
-            load.wait()
-    probe[...] = probe_raw[...].astype(jnp.float32)
-    with jax.named_scope("w_barrier"):
-        pl.semaphore_wait(barrier, greetings)
+        wait_bytes(rows_in.at[own], local_sem.at[0])
+        wait_bytes(spots_in.at[own], local_sem.at[1])
 
     parts = (rows_in, spots_in)
 
-    def patch_copies(k, m):
-        there = lax.rem(d + k, dp_count)
-        later = c if m == 0 else 2 * m + side
-        return [
-            pltpu.make_async_remote_copy(
-                src_ref=part.at[c, d],
-                dst_ref=part.at[c, d],
-                send_sem=patch_send.at[k, m, kind],
-                recv_sem=patch_recv.at[c, d, kind],
-                device_id=(there, later, t),
-                device_id_type=MESH,
-            )
-            for kind, part in enumerate(parts)
-        ]
-
-    def for_patches(act):
-        for k in range(1, dp_count):
-            for copy in patch_copies(k, 0):
-                act(copy)
-        for k in range(dp_count):
-            for m in range(1, chips):
-
-                @pl.when(chip < m)
-                def _():
-                    for copy in patch_copies(k, m):
-                        act(copy)
-
-    def pass_copies(block):
-        return [
-            pltpu.make_async_remote_copy(
-                src_ref=part.at[block],
-                dst_ref=part.at[block],
-                send_sem=pass_send.at[block, kind],
-                recv_sem=pass_recv.at[block, kind],
-                device_id=(d, partner, t),
-                device_id_type=MESH,
-            )
-            for kind, part in enumerate(parts)
-        ]
-
-    def text_copy(m, group):
-        return pltpu.make_async_remote_copy(
-            src_ref=text.at[c, group],
-            dst_ref=text.at[c, group],
-            send_sem=text_send.at[m, group],
-            recv_sem=text_recv.at[c, group],
-            device_id=(d, 2 * m + side, t),
-            device_id_type=MESH,
-        )
-
-    def relay_copy(block, group):
+    def send_patches(there, last_block):
+        def to_block(number, carry):
+            for kind, part in enumerate(parts):
+                pltpu.make_async_remote_copy(
+                    src_ref=part.at[own],
+                    dst_ref=part.at[own],
+                    send_sem=patch_send.at[kind],
+                    recv_sem=patch_recv.at[c, kind],
+                    device_id=(there, ctx_count - 1 - number, t),
+                    device_id_type=MESH,
+                ).start()
+            return carry
+
+        lax.fori_loop(0, ctx_count - last_block, to_block, 0)
+
+    def send_down(there, carry):
+        send_patches(there, c)
+        return carry
+
+    with jax.named_scope("down"):
+        lax.fori_loop(0, d, send_down, 0)
+        send_patches(d, c + 1)
+    with jax.named_scope("w_text"):
+        for group in range(groups):
+            wait_bytes(text.at[c, group], text_recv.at[c, group])
+
+    def text_copy(group, block, there, sem):
         return pltpu.make_async_remote_copy(
             src_ref=text.at[block, group],
             dst_ref=text.at[block, group],
-            send_sem=relay_send.at[block, group],
+            send_sem=sem,
             recv_sem=text_recv.at[block, group],
-            device_id=(d, partner, t),
+            device_id=(d, there, t),
             device_id_type=MESH,
         )
 
-    def for_text(act):
+    with jax.named_scope("texts"):
         for group in range(groups):
-            for m in range(1, chips):
-
-                @pl.when(chip < m)
-                def _():
-                    act(text_copy(m, group))
-
-    def relays(block):
-        return (block < c + 1 - side) & (side == block % 2)
-
-    with jax.named_scope("starts"):
-        for_patches(lambda copy: copy.start())
-        for_text(lambda copy: copy.start())
-
-    def wait_patches(block):
-        for k in range(1, dp_count):
-            there = lax.rem(d + k, dp_count)
-            for kind, part in enumerate(parts):
-                pltpu.make_async_remote_copy(
-                    src_ref=part.at[block, there],
-                    dst_ref=part.at[block, there],
-                    send_sem=patch_send.at[k, 0, kind],
-                    recv_sem=patch_recv.at[block, there, kind],
-                    device_id=(there, c, t),
-                    device_id_type=MESH,
-                ).wait_recv()
-
-    def wait_own_patches(block):
-        for kind, part in enumerate(parts):
-            pltpu.make_async_remote_copy(
-                src_ref=part.at[block, d],
-                dst_ref=part.at[block, d],
-                send_sem=patch_send.at[0, 0, kind],
-                recv_sem=patch_recv.at[block, d, kind],
-                device_id=(d, partner, t),
-                device_id_type=MESH,
-            ).wait_recv()
+
+            def to_chip(m, carry):
+                text_copy(group, c, 2 * m + 1, text_send).start()
+                return carry
+
+            lax.fori_loop(chip + side, chips, to_chip, 0)
+    load_probe.wait()
+    probe[...] = probe_raw[...].astype(jnp.float32)
+
+    def send_up(there, carry):
+        pl.semaphore_wait(ready.at[there], ctx_count - c)
+        send_patches(there, c)
+        return carry
+
+    def relay(group):
+        def hand_on(block, carry):
+            wait_bytes(text.at[block, group], text_recv.at[block, group])
+            text_copy(group, block, c - 1, relay_send).start()
+            return carry
+
+        lax.fori_loop(0, (c - 1) * side, hand_on, 0)
+
+    split = jnp.maximum(d + 1, dp_count - 1)
+    with jax.named_scope("up1"):
+        lax.fori_loop(d + 1, split, send_up, 0)
+    with jax.named_scope("relay1"):
+        relay(0)
+    with jax.named_scope("up2"):
+        lax.fori_loop(split, dp_count, send_up, 0)
+    with jax.named_scope("relay2"):
+        for group in range(1, groups):
+            relay(group)
+
+    def out_copy(group):
+        width = queries.shape[1] // groups
+        place = pl.ds(pl.multiple_of(group * width, width), width)
+        return copy_of(out.at[:, place], out_any.at[:, place], out_sem)
 
     def merge(block):
-        slots = dp_count * rows_hbm.shape[0]
-        spots = spots_in[block]
+        slots = dp_count * row_count
+        span = slice(block * dp_count, (block + 1) * dp_count)
+        spots = spots_in[span]
         code = spots[:, 0] * token_count + spots[:, 1]
         code = jnp.concatenate([code[k] for k in range(dp_count)], axis=1)
         here = d * token_count + lax.broadcasted_iota(jnp.int32, (token_count, slots), 0)
         landing = jnp.where(code == here, 1.0, 0.0).astype(jnp.bfloat16)
-        rows = rows_in[block].astype(jnp.float32)
-        span = pl.ds(block * token_count, token_count)
+        rows = rows_in[span].astype(jnp.float32)
+        tokens = slice(block * token_count, (block + 1) * token_count)
         for kind in range(2):
             kind_rows = rows[:, :, kind, :].reshape(slots, kv_width).astype(jnp.bfloat16)
             arrivals = jnp.dot(landing, kind_rows, preferred_element_type=jnp.float32)
             for group in range(groups):
                 whole = text[block, group, kind].astype(jnp.float32) + arrivals[:, lanes(group)]
                 if kind == 0:
-                    merged_keys[group, span, :] = whole.astype(jnp.bfloat16)
+                    merged_keys[group, tokens, :] = whole.astype(jnp.bfloat16)
                 else:
-                    merged_values[group, span, 0:HD] = whole.astype(jnp.bfloat16)
-
-    with jax.named_scope("patches"):
-        for block in range(ctx_count):
-
-            @pl.when((block <= c) & (side == block % 2))
-            def _():
-                wait_patches(block)
-
-                @pl.when(block < c)
-                def _():
-                    wait_own_patches(block)
-
-                @pl.when(relays(block))
-                def _():
-                    for copy in pass_copies(block):
-                        copy.start()
-
-    with jax.named_scope("own"):
-
-        @pl.when(side == 0)
-        def _():
+                    merged_values[group, tokens, 0:HD] = whole.astype(jnp.bfloat16)
+
+    def attend(last):
+        with jax.named_scope("w_patch"):
+            for block in range(last + 1):
+                senders = dp_count if block < last else dp_count - 1
+                for kind, part in enumerate(parts):
+                    wait_bytes(
+                        part.at[pl.ds(block * dp_count, senders)], patch_recv.at[block, kind]
+                    )
+        with jax.named_scope("w_kv"):
+            first = max(last - 1, 0) if last % 2 else 0
             for group in range(groups):
-                relay_copy(c, group).start()
-
-        for block in range(ctx_count):
-
-            @pl.when(block == c)
-            def _():
+                for block in range(first, last):
+                    wait_bytes(text.at[block, group], text_recv.at[block, group])
+        with jax.named_scope("merge"):
+            for block in range(last + 1):
                 merge(block)
-
-    with jax.named_scope("relay"):
-        for group in range(groups):
-            for block in range(ctx_count - 2):
-
-                @pl.when((block < c - side) & (side == block % 2))
-                def _():
-                    relay_copy(block, group).wait_recv()
-                    relay_copy(block, group).start()
-
-    with jax.named_scope("merges"):
-        for block in range(ctx_count - 1):
-
-            @pl.when((block < c) & (side != block % 2))
-            def _():
-                for copy in pass_copies(block):
-                    copy.wait_recv()
-                for group in range(groups):
-                    relay_copy(block, group).wait_recv()
-                merge(block)
-
-            if block < ctx_count - 2:
-
-                @pl.when((block < c) & (side == block % 2))
-                def _():
-                    merge(block)
-
-    load_queries.wait()
-
-    def out_copy(group):
-        width = queries.shape[1] // groups
-        place = pl.ds(pl.multiple_of(group * width, width), width)
-        return pltpu.make_async_copy(out.at[:, place], out_any.at[:, place], out_sem.at[group])
-
-    def attend(last):
+        load_queries.wait()
+
         def step(group, total):
             total = total + attend_rows(
                 queries, merged_keys, merged_values, probe, out, heads, group, last, token_count
@@ -435,15 +384,15 @@
             out_copy(group).start()
             return total
 
-        total = lax.fori_loop(0, groups, step, jnp.zeros((token_count, HD), jnp.float32))
-        partial[...] = jnp.sum(jnp.transpose(total), axis=0, keepdims=True)
-
-    with jax.named_scope("attend"):
-        for last in range(ctx_count):
-
-            @pl.when(c == last)
-            def _():
-                attend(last)
+        with jax.named_scope("attend"):
+            total = lax.fori_loop(0, groups, step, jnp.zeros((token_count, HD), jnp.float32))
+            partial[...] = jnp.sum(jnp.transpose(total), axis=0, keepdims=True)
+
+    for last in range(ctx_count):
+
+        @pl.when(c == last)
+        def _():
+            attend(last)
 
     value_copies = [
         pltpu.make_async_remote_copy(
@@ -459,19 +408,21 @@
     for copy in value_copies:
         copy.start()
     with jax.named_scope("tail"):
-        for_patches(lambda copy: copy.wait_send())
-        for_text(lambda copy: copy.wait_send())
-        for block in range(ctx_count):
-
-            @pl.when(relays(block))
+        for last in range(ctx_count):
+
+            @pl.when(c == last)
             def _():
-                for copy in pass_copies(block):
-                    copy.wait_send()
-                for group in range(groups):
-                    relay_copy(block, group).wait_send()
-
-        for group in range(groups):
-            out_copy(group).wait()
+                sent = dp_count * (ctx_count - last) - 1
+                if sent:
+                    for kind, part in enumerate(parts):
+                        wait_bytes(part.at[pl.ds(0, sent)], patch_send.at[kind])
+                chips_after = chips - last // 2 - last % 2
+                if chips_after:
+                    wait_bytes(text.at[pl.ds(0, chips_after)], text_send)
+                if last % 2 and last > 1:
+                    wait_bytes(text.at[pl.ds(0, last - 1)], relay_send)
+
+        wait_bytes(out, out_sem)
         for copy in value_copies:
             copy.wait()
     whole = partial[...]
@@ -530,8 +481,8 @@
             pltpu.VMEM((token_count, query_width), jnp.bfloat16),
             pltpu.VMEM((token_count, query_width), jnp.bfloat16),
             pltpu.VMEM((ctx_count, groups, 2, token_count, HD), jnp.bfloat16),
-            pltpu.VMEM((ctx_count, dp_count, row_count, 2, kv_width), jnp.bfloat16),
-            pltpu.VMEM((ctx_count, dp_count, 2, 1, row_count), jnp.int32),
+            pltpu.VMEM((ctx_count * dp_count, row_count, 2, kv_width), jnp.bfloat16),
+            pltpu.VMEM((ctx_count * dp_count, 2, 1, row_count), jnp.int32),
             pltpu.VMEM((groups, ctx_count * token_count, HD), jnp.bfloat16),
             pltpu.VMEM((groups, ctx_count * token_count, 2 * HD), jnp.bfloat16),
             pltpu.VMEM((heads, HD), jnp.bfloat16),
@@ -539,17 +490,16 @@
             pltpu.VMEM((1, token_count), jnp.float32),
             pltpu.VMEM((others, 1, token_count), jnp.float32),
             dma,
-            dma((groups,)),
-            dma((4 + 2 * groups,)),
-            dma((ctx_count // 2, groups)),
+            dma,
+            dma((3,)),
+            dma,
             dma((ctx_count, groups)),
-            dma((ctx_count, groups)),
-            dma((dp_count, ctx_count // 2, 2)),
-            dma((ctx_count, dp_count, 2)),
-            dma((ctx_count, 2)),
+            dma,
+            dma((2,)),
             dma((ctx_count, 2)),
             dma((others,)),
             dma((others,)),
+            pltpu.SemaphoreType.REGULAR((dp_count,)),
         ],
         compiler_params=pltpu.CompilerParams(
             collective_id=0, has_side_effects=True, vmem_limit_bytes=24 * 2**20

time: 18.2 us -> 15.9 us (0.87)
  the two profiles are of different devices: /device:TPU:5 before, /device:TPU:28 now
where the time goes in v2:
time: 15.9 us; the launch traced here: 15.8 us
  Pallas kernels  15.1 us (95%)
  between operations  0.64 us (4%)
    pallas_call x1, Pallas kernels, fused_body(): pl.pallas_call(functools.partial(fused_kernel, sizes), out_shape=shapes,...  14.3 us
    pallas_call x1, Pallas kernels, fused_body(): pl.pallas_call(write_kernel, out_shape=shapes, in_specs=[anywhere] * 2, o...  0.83 us

profile of v2, /device:TPU:28, one launch (start us, length us, event | category | flops | bytes accessed | tf_op | source)
XLA Modules:
  0.0 15.8 jit_solution(17696122070454395159)
XLA Ops:
  0.6 14.3 %merged_attention.1 = (bf16[128,2048]{1,0:T(8,128)(2,1)S(1)}, f32[1,128]{1,0:T(1,128)S(1)}) custom-call(s32[1,8]{1,0:T(1,128)} %bitcast.13, s32[1,8]{1,0:T(1,128)} %bitcast.14, bf16[8,2,256]{2,1,0:T(2,128)(2,1)} %bitcast.11, bf16[128,256]{1,0:T(8,128)(2,1)} %bitcast.9, bf16[128,256]{1,0:T(8,128)(2,1)} %bitcast.10, bf16[16,128]{1,0:T(8,128)(2,1)} %bitcast.12, ...), custom_call_target="tpu_custom_call" | custom-call | tf_op jit(solution)/shard_map/merged_attention/pallas_call | solution.py:475
  14.9 0.8 %write_out.1 = (bf16[128,2048]{1,0:T(8,128)(2,1)}, f32[1,128]{1,0:T(1,128)}) custom-call(bf16[128,2048]{1,0:T(8,128)(2,1)S(1)} %get-tuple-element.6.attention, f32[1,128]{1,0:T(1,128)S(1)} %get-tuple-element.7.value), custom_call_target="tpu_custom_call" | custom-call | tf_op jit(solution)/shard_map/write_out/pallas_call | solution.py:509

commit v3 on v2

--- a/solution.py
+++ b/solution.py
@@ -119,21 +119,22 @@
     return (attention[None], value_out[None])
 
 
-def attend_rows(queries, merged_keys, merged_values, probe, out, heads, group, last, token_count):
-    group_size = heads // merged_keys.shape[0]
-    first = group * group_size
+def attend(queries, merged_keys, merged_values, probe, out, last, group, totals):
+    token_count, width = queries.shape
+    groups = merged_keys.shape[0]
+    group_size = width // HD // groups
     length = (last + 1) * token_count
-    rows = math.gcd(token_count, 32)
+    rows = token_count // len(totals)
     score_scale = HD ** (-0.5) * math.log2(math.e)
+    heads = range(group * group_size, (group + 1) * group_size)
     block_keys = merged_keys[group, 0:length, :]
     block_values = merged_values[group, 0:length, :]
-    places = [
-        pl.ds(pl.multiple_of((first + extra) * HD, HD), HD) for extra in range(group_size)
-    ]
-    totals = []
-    for lower in range(0, token_count, rows):
+    for number in range(len(totals)):
+        lower = number * rows
         span = slice(lower, lower + rows)
-        stacked = jnp.concatenate([queries[span, place] for place in places], axis=0)
+        stacked = jnp.concatenate(
+            [queries[span, head * HD : (head + 1) * HD] for head in heads], axis=0
+        )
         scores = lax.dot_general(
             stacked, block_keys, (((1,), (1,)), ((), ())), preferred_element_type=jnp.float32
         )
@@ -147,13 +148,12 @@
         rounded = jnp.concatenate([w.astype(jnp.bfloat16) for w in weights], axis=1)
         sums = jnp.dot(rounded, block_values, preferred_element_type=jnp.float32)
         result = (sums[:, :HD] * (1.0 / sums[:, HD:])).astype(jnp.bfloat16)
-        total = jnp.zeros((rows, HD), jnp.float32)
-        for extra in range(group_size):
+        for extra, head in enumerate(heads):
             piece = result[extra * rows : (extra + 1) * rows]
-            out[span, places[extra]] = piece
-            total = total + piece.astype(jnp.float32) * probe[pl.ds(first + extra, 1), :]
-        totals.append(total)
-    return jnp.concatenate(totals, axis=0)
+            out[span, head * HD : (head + 1) * HD] = piece
+            totals[number] = (
+                totals[number] + piece.astype(jnp.float32) * probe[head : head + 1, :]
+            )
 
 
 def fused_kernel(
@@ -186,6 +186,7 @@
     relay_send,
     patch_send,
     patch_recv,
+    pass_send,
     value_send,
     value_recv,
     ready,
@@ -201,21 +202,26 @@
     chip = c // 2
 
     barrier = pltpu.get_barrier_semaphore()
-
-    def greet(device):
+    in_pair = dp_count
+
+    def greet(*device):
         pl.semaphore_signal(barrier, inc=1, device_id=device, device_id_type=MESH)
 
-    for m in range(1, ctx_count):
-        greet((d, lax.rem(c + m, ctx_count), t))
-    for k in range(1, tp_count):
-        greet((d, c, lax.rem(t + k, tp_count)))
-
-    def greet_above(there, carry):
+    def over(lower, upper, act):
+        def step(number, carry):
+            act(number)
+            return carry
+
+        lax.fori_loop(lower, upper, step, 0)
+
+    over(1, ctx_count, lambda step: greet(d, lax.rem(c + step, ctx_count), t))
+    over(t + 1, tp_count, lambda other: greet(d, c, other))
+
+    def greet_plane(there):
         for block in range(ctx_count):
-            greet((there, block, t))
-        return carry
-
-    lax.fori_loop(d + 1, dp_count, greet_above, 0)
+            greet(there, block, t)
+
+    over(d + 1, dp_count, greet_plane)
 
     def lanes(group):
         return slice(group * HD, (group + 1) * HD)
@@ -245,46 +251,44 @@
     load_queries.start()
     merged_values[:, :, HD:] = jnp.ones((groups, ctx_count * token_count, HD), jnp.bfloat16)
     with jax.named_scope("w_barrier"):
-        pl.semaphore_wait(barrier, ctx_count - 1 + tp_count - 1 + d * ctx_count)
-
-    def announce(there, carry):
-        def to_block(block, inner):
-            pl.semaphore_signal(
-                ready.at[d], inc=1, device_id=(there, block, t), device_id_type=MESH
-            )
-            return inner
-
-        return lax.fori_loop(0, c + 1, to_block, carry)
-
-    lax.fori_loop(0, d, announce, 0)
+        pl.semaphore_wait(barrier, d * ctx_count + ctx_count - 1 + t)
+
+    def announce(number, *device):
+        pl.semaphore_signal(
+            ready.at[number], inc=1, device_id=device, device_id_type=MESH
+        )
+
+    over(
+        0,
+        d,
+        lambda there: over(c * side, c + 1, lambda block: announce(d, there, block, t)),
+    )
+    over(0, t, lambda other: announce(in_pair, d, c, other))
     with jax.named_scope("w_loads"):
         wait_bytes(rows_in.at[own], local_sem.at[0])
         wait_bytes(spots_in.at[own], local_sem.at[1])
 
     parts = (rows_in, spots_in)
 
-    def send_patches(there, last_block):
-        def to_block(number, carry):
+    def send_patches(there, own_block):
+        def to_block(block):
             for kind, part in enumerate(parts):
                 pltpu.make_async_remote_copy(
                     src_ref=part.at[own],
                     dst_ref=part.at[own],
                     send_sem=patch_send.at[kind],
                     recv_sem=patch_recv.at[c, kind],
-                    device_id=(there, ctx_count - 1 - number, t),
+                    device_id=(there, block, t),
                     device_id_type=MESH,
                 ).start()
-            return carry
-
-        lax.fori_loop(0, ctx_count - last_block, to_block, 0)
-
-    def send_down(there, carry):
-        send_patches(there, c)
-        return carry
+
+        over(0, chips - 1 - chip, lambda number: to_block(2 * (chips - 1 - number)))
+        if own_block:
+            to_block(c)
 
     with jax.named_scope("down"):
-        lax.fori_loop(0, d, send_down, 0)
-        send_patches(d, c + 1)
+        over(0, d, lambda there: send_patches(there, True))
+    send_patches(d, False)
     with jax.named_scope("w_text"):
         for group in range(groups):
             wait_bytes(text.at[c, group], text_recv.at[c, group])
@@ -301,45 +305,45 @@
 
     with jax.named_scope("texts"):
         for group in range(groups):
-
-            def to_chip(m, carry):
-                text_copy(group, c, 2 * m + 1, text_send).start()
-                return carry
-
-            lax.fori_loop(chip + side, chips, to_chip, 0)
+            over(
+                chip + side,
+                chips,
+                lambda m: text_copy(group, c, 2 * m + 1, text_send).start(),
+            )
+
     load_probe.wait()
     probe[...] = probe_raw[...].astype(jnp.float32)
 
-    def send_up(there, carry):
-        pl.semaphore_wait(ready.at[there], ctx_count - c)
-        send_patches(there, c)
-        return carry
+    def send_up(there):
+        pl.semaphore_wait(ready.at[there], chips - chip)
+        send_patches(there, True)
 
     def relay(group):
-        def hand_on(block, carry):
+        def hand_on(block):
             wait_bytes(text.at[block, group], text_recv.at[block, group])
             text_copy(group, block, c - 1, relay_send).start()
-            return carry
-
-        lax.fori_loop(0, (c - 1) * side, hand_on, 0)
-
-    split = jnp.maximum(d + 1, dp_count - 1)
-    with jax.named_scope("up1"):
-        lax.fori_loop(d + 1, split, send_up, 0)
-    with jax.named_scope("relay1"):
-        relay(0)
-    with jax.named_scope("up2"):
-        lax.fori_loop(split, dp_count, send_up, 0)
-    with jax.named_scope("relay2"):
-        for group in range(1, groups):
+
+        over(0, (c - 1) * side, hand_on)
+
+    with jax.named_scope("up"):
+        over(d + 1, dp_count, send_up)
+    with jax.named_scope("relay"):
+        for group in range(groups):
             relay(group)
 
-    def out_copy(group):
-        width = queries.shape[1] // groups
-        place = pl.ds(pl.multiple_of(group * width, width), width)
-        return copy_of(out.at[:, place], out_any.at[:, place], out_sem)
-
-    def merge(block):
+    def pass_patches(block):
+        span = pl.ds(block * dp_count, dp_count)
+        for kind, part in enumerate(parts):
+            pltpu.make_async_remote_copy(
+                src_ref=part.at[span],
+                dst_ref=part.at[span],
+                send_sem=pass_send.at[kind],
+                recv_sem=patch_recv.at[block, kind],
+                device_id=(d, c + 1, t),
+                device_id_type=MESH,
+            ).start()
+
+    def merge(block, chosen):
         slots = dp_count * row_count
         span = slice(block * dp_count, (block + 1) * dp_count)
         spots = spots_in[span]
@@ -347,19 +351,20 @@
         code = jnp.concatenate([code[k] for k in range(dp_count)], axis=1)
         here = d * token_count + lax.broadcasted_iota(jnp.int32, (token_count, slots), 0)
         landing = jnp.where(code == here, 1.0, 0.0).astype(jnp.bfloat16)
-        rows = rows_in[span].astype(jnp.float32)
+        wide = slice(chosen[0] * HD, (chosen[-1] + 1) * HD)
+        rows = rows_in[span, :, :, wide].astype(jnp.float32)
         tokens = slice(block * token_count, (block + 1) * token_count)
         for kind in range(2):
-            kind_rows = rows[:, :, kind, :].reshape(slots, kv_width).astype(jnp.bfloat16)
+            kind_rows = rows[:, :, kind, :].reshape(slots, -1).astype(jnp.bfloat16)
             arrivals = jnp.dot(landing, kind_rows, preferred_element_type=jnp.float32)
-            for group in range(groups):
-                whole = text[block, group, kind].astype(jnp.float32) + arrivals[:, lanes(group)]
+            for number, group in enumerate(chosen):
+                whole = text[block, group, kind].astype(jnp.float32) + arrivals[:, lanes(number)]
                 if kind == 0:
                     merged_keys[group, tokens, :] = whole.astype(jnp.bfloat16)
                 else:
                     merged_values[group, tokens, 0:HD] = whole.astype(jnp.bfloat16)
 
-    def attend(last):
+    def finish(last):
         with jax.named_scope("w_patch"):
             for block in range(last + 1):
                 senders = dp_count if block < last else dp_count - 1
@@ -367,32 +372,38 @@
                     wait_bytes(
                         part.at[pl.ds(block * dp_count, senders)], patch_recv.at[block, kind]
                     )
-        with jax.named_scope("w_kv"):
-            first = max(last - 1, 0) if last % 2 else 0
-            for group in range(groups):
-                for block in range(first, last):
+                if last % 2 == 0:
+                    pass_patches(block)
+        odd = last % 2
+        whole = odd or last == 0
+        rows = math.gcd(token_count, 16 if odd else 64)
+        totals = [jnp.zeros((rows, HD), jnp.float32)] * (token_count // rows)
+        load_queries.wait()
+
+        def compute(chosen):
+            for block in range(last + 1):
+                merge(block, chosen)
+            for group in chosen:
+                attend(queries, merged_keys, merged_values, probe, out, last, group, totals)
+
+        for group in range(groups):
+            with jax.named_scope("w_kv%d" % group):
+                for block in range(last - 1 if odd else 0, last):
                     wait_bytes(text.at[block, group], text_recv.at[block, group])
-        with jax.named_scope("merge"):
-            for block in range(last + 1):
-                merge(block)
-        load_queries.wait()
-
-        def step(group, total):
-            total = total + attend_rows(
-                queries, merged_keys, merged_values, probe, out, heads, group, last, token_count
-            )
-            out_copy(group).start()
-            return total
-
-        with jax.named_scope("attend"):
-            total = lax.fori_loop(0, groups, step, jnp.zeros((token_count, HD), jnp.float32))
-            partial[...] = jnp.sum(jnp.transpose(total), axis=0, keepdims=True)
+            if not whole:
+                with jax.named_scope("attend%d" % group):
+                    compute((group,))
+        if whole:
+            with jax.named_scope("attend"):
+                compute(range(groups))
+        total = jnp.concatenate(totals, axis=0)
+        partial[...] = jnp.sum(jnp.transpose(total), axis=0, keepdims=True)
 
     for last in range(ctx_count):
 
         @pl.when(c == last)
         def _():
-            attend(last)
+            finish(last)
 
     value_copies = [
         pltpu.make_async_remote_copy(
@@ -405,24 +416,36 @@
         )
         for k in range(1, tp_count)
     ]
+    with jax.named_scope("w_pair"):
+
+        @pl.when(t < tp_count - 1)
+        def _():
+            pl.semaphore_wait(ready.at[in_pair], tp_count - 1 - t)
+
     for copy in value_copies:
         copy.start()
+    store = copy_of(out, out_any, out_sem)
+    store.start()
     with jax.named_scope("tail"):
         for last in range(ctx_count):
 
             @pl.when(c == last)
             def _():
-                sent = dp_count * (ctx_count - last) - 1
+                later = chips - 1 - last // 2
+                sent = dp_count * (later + 1) - 1
                 if sent:
                     for kind, part in enumerate(parts):
                         wait_bytes(part.at[pl.ds(0, sent)], patch_send.at[kind])
-                chips_after = chips - last // 2 - last % 2
-                if chips_after:
-                    wait_bytes(text.at[pl.ds(0, chips_after)], text_send)
+                copies = later + 1 - last % 2
+                if copies:
+                    wait_bytes(text.at[pl.ds(0, copies)], text_send)
                 if last % 2 and last > 1:
                     wait_bytes(text.at[pl.ds(0, last - 1)], relay_send)
-
-        wait_bytes(out, out_sem)
+                if last % 2 == 0:
+                    for kind, part in enumerate(parts):
+                        wait_bytes(part.at[pl.ds(0, (last + 1) * dp_count)], pass_send.at[kind])
+
+        store.wait()
         for copy in value_copies:
             copy.wait()
     whole = partial[...]
@@ -497,9 +520,10 @@
             dma,
             dma((2,)),
             dma((ctx_count, 2)),
+            dma((2,)),
             dma((others,)),
             dma((others,)),
-            pltpu.SemaphoreType.REGULAR((dp_count,)),
+            pltpu.SemaphoreType.REGULAR((dp_count + 1,)),
         ],
         compiler_params=pltpu.CompilerParams(
             collective_id=0, has_side_effects=True, vmem_limit_bytes=24 * 2**20

time: 15.9 us -> 14.8 us (0.931)
  Pallas kernels: 15.1 us -> 14 us
    pallas_call x1, Pallas kernels: 14.3 us -> 13.2 us  [fused_body(): pl.pallas_call(functools.partial(fused_kernel, sizes), out_shape=shapes,...]
where the time goes in v3:
time: 14.8 us; the launch traced here: 14.7 us
  Pallas kernels  14 us (95%)
  between operations  0.64 us (4%)
    pallas_call x1, Pallas kernels, fused_body(): pl.pallas_call(functools.partial(fused_kernel, sizes), out_shape=shapes,...  13.2 us
    pallas_call x1, Pallas kernels, fused_body(): pl.pallas_call(write_kernel, out_shape=shapes, in_specs=[anywhere] * 2, o...  0.83 us

profile of v3, /device:TPU:28, one launch (start us, length us, event | category | flops | bytes accessed | tf_op | source)
XLA Modules:
  0.0 14.7 jit_solution(10075280363902496130)
XLA Ops:
  0.6 13.2 %merged_attention.1 = (bf16[128,2048]{1,0:T(8,128)(2,1)S(1)}, f32[1,128]{1,0:T(1,128)S(1)}) custom-call(s32[1,8]{1,0:T(1,128)} %bitcast.13, s32[1,8]{1,0:T(1,128)} %bitcast.14, bf16[8,2,256]{2,1,0:T(2,128)(2,1)} %bitcast.11, bf16[128,256]{1,0:T(8,128)(2,1)} %bitcast.9, bf16[128,256]{1,0:T(8,128)(2,1)} %bitcast.10, bf16[16,128]{1,0:T(8,128)(2,1)} %bitcast.12, ...), custom_call_target="tpu_custom_call" | custom-call | tf_op jit(solution)/shard_map/merged_attention/pallas_call | solution.py:498
  13.9 0.8 %write_out.1 = (bf16[128,2048]{1,0:T(8,128)(2,1)}, f32[1,128]{1,0:T(1,128)}) custom-call(bf16[128,2048]{1,0:T(8,128)(2,1)S(1)} %get-tuple-element.6.attention, f32[1,128]{1,0:T(1,128)S(1)} %get-tuple-element.7.value), custom_call_target="tpu_custom_call" | custom-call | tf_op jit(solution)/shard_map/write_out/pallas_call | solution.py:533

commit v4 on v3

--- a/solution.py
+++ b/solution.py
@@ -128,7 +128,8 @@
     score_scale = HD ** (-0.5) * math.log2(math.e)
     heads = range(group * group_size, (group + 1) * group_size)
     block_keys = merged_keys[group, 0:length, :]
-    block_values = merged_values[group, 0:length, :]
+    summed = len(totals) > 1
+    block_values = merged_values[group, 0:length, 0 : 2 * HD if summed else HD]
     for number in range(len(totals)):
         lower = number * rows
         span = slice(lower, lower + rows)
@@ -147,7 +148,11 @@
         weights = [jnp.exp2((part - top) * score_scale) for part in parts]
         rounded = jnp.concatenate([w.astype(jnp.bfloat16) for w in weights], axis=1)
         sums = jnp.dot(rounded, block_values, preferred_element_type=jnp.float32)
-        result = (sums[:, :HD] * (1.0 / sums[:, HD:])).astype(jnp.bfloat16)
+        if summed:
+            denominator = sums[:, HD:]
+        else:
+            denominator = jnp.sum(functools.reduce(jnp.add, weights), axis=1, keepdims=True)
+        result = (sums[:, :HD] * (1.0 / denominator)).astype(jnp.bfloat16)
         for extra, head in enumerate(heads):
             piece = result[extra * rows : (extra + 1) * rows]
             out[span, head * HD : (head + 1) * HD] = piece
@@ -200,6 +205,7 @@
     chips = ctx_count // 2
     side = lax.rem(c, 2)
     chip = c // 2
+    partner = c + 1 - 2 * side
 
     barrier = pltpu.get_barrier_semaphore()
     in_pair = dp_count
@@ -261,7 +267,7 @@
     over(
         0,
         d,
-        lambda there: over(c * side, c + 1, lambda block: announce(d, there, block, t)),
+        lambda there: over(c * (1 - side), c + 1, lambda block: announce(d, there, block, t)),
     )
     over(0, t, lambda other: announce(in_pair, d, c, other))
     with jax.named_scope("w_loads"):
@@ -269,6 +275,7 @@
         wait_bytes(spots_in.at[own], local_sem.at[1])
 
     parts = (rows_in, spots_in)
+    targets = chips - chip - side
 
     def send_patches(there, own_block):
         def to_block(block):
@@ -282,9 +289,9 @@
                     device_id_type=MESH,
                 ).start()
 
-        over(0, chips - 1 - chip, lambda number: to_block(2 * (chips - 1 - number)))
         if own_block:
             to_block(c)
+        over(chip + side, chips, lambda m: to_block(2 * m + 1))
 
     with jax.named_scope("down"):
         over(0, d, lambda there: send_patches(there, True))
@@ -305,25 +312,30 @@
 
     with jax.named_scope("texts"):
         for group in range(groups):
+            hub = (group + 1) % 2
             over(
-                chip + side,
-                chips,
-                lambda m: text_copy(group, c, 2 * m + 1, text_send).start(),
+                chip + 1, chips, lambda m: text_copy(group, c, 2 * m + hub, text_send).start()
             )
+
+            @pl.when(side == 0)
+            def _():
+                text_copy(group, c, c + 1, text_send).start()
 
     load_probe.wait()
     probe[...] = probe_raw[...].astype(jnp.float32)
 
     def send_up(there):
-        pl.semaphore_wait(ready.at[there], chips - chip)
+        pl.semaphore_wait(ready.at[there], targets + 1)
         send_patches(there, True)
 
     def relay(group):
         def hand_on(block):
             wait_bytes(text.at[block, group], text_recv.at[block, group])
-            text_copy(group, block, c - 1, relay_send).start()
-
-        over(0, (c - 1) * side, hand_on)
+            text_copy(group, block, partner, relay_send.at[group]).start()
+
+        @pl.when(side == (group + 1) % 2)
+        def _():
+            over(0, 2 * chip, hand_on)
 
     with jax.named_scope("up"):
         over(d + 1, dp_count, send_up)
@@ -339,7 +351,7 @@
                 dst_ref=part.at[span],
                 send_sem=pass_send.at[kind],
                 recv_sem=patch_recv.at[block, kind],
-                device_id=(d, c + 1, t),
+                device_id=(d, c - 1, t),
                 device_id_type=MESH,
             ).start()
 
@@ -372,30 +384,21 @@
                     wait_bytes(
                         part.at[pl.ds(block * dp_count, senders)], patch_recv.at[block, kind]
                     )
-                if last % 2 == 0:
+                if last % 2 and block < last - 1:
                     pass_patches(block)
-        odd = last % 2
-        whole = odd or last == 0
-        rows = math.gcd(token_count, 16 if odd else 64)
-        totals = [jnp.zeros((rows, HD), jnp.float32)] * (token_count // rows)
-        load_queries.wait()
-
-        def compute(chosen):
+        with jax.named_scope("w_kv"):
+            for group in range(groups):
+                relayed = 0 if last % 2 != (group + 1) % 2 else 2 * (last // 2)
+                for block in range(relayed, last):
+                    wait_bytes(text.at[block, group], text_recv.at[block, group])
+            load_queries.wait()
+        with jax.named_scope("attend"):
+            rows = math.gcd(token_count, 16) if last % 2 and last > 1 else token_count
+            totals = [jnp.zeros((rows, HD), jnp.float32)] * (token_count // rows)
             for block in range(last + 1):
-                merge(block, chosen)
-            for group in chosen:
+                merge(block, range(groups))
+            for group in range(groups):
                 attend(queries, merged_keys, merged_values, probe, out, last, group, totals)
-
-        for group in range(groups):
-            with jax.named_scope("w_kv%d" % group):
-                for block in range(last - 1 if odd else 0, last):
-                    wait_bytes(text.at[block, group], text_recv.at[block, group])
-            if not whole:
-                with jax.named_scope("attend%d" % group):
-                    compute((group,))
-        if whole:
-            with jax.named_scope("attend"):
-                compute(range(groups))
         total = jnp.concatenate(totals, axis=0)
         partial[...] = jnp.sum(jnp.transpose(total), axis=0, keepdims=True)
 
@@ -431,19 +434,18 @@
 
             @pl.when(c == last)
             def _():
-                later = chips - 1 - last // 2
-                sent = dp_count * (later + 1) - 1
-                if sent:
-                    for kind, part in enumerate(parts):
+                sent = dp_count * (chips - last // 2 - last % 2 + 1) - 1
+                for kind, part in enumerate(parts):
+                    if sent:
                         wait_bytes(part.at[pl.ds(0, sent)], patch_send.at[kind])
-                copies = later + 1 - last % 2
+                    if last % 2 and last > 1:
+                        wait_bytes(part.at[pl.ds(0, (last - 1) * dp_count)], pass_send.at[kind])
+                copies = chips - last // 2 - last % 2
                 if copies:
                     wait_bytes(text.at[pl.ds(0, copies)], text_send)
-                if last % 2 and last > 1:
-                    wait_bytes(text.at[pl.ds(0, last - 1)], relay_send)
-                if last % 2 == 0:
-                    for kind, part in enumerate(parts):
-                        wait_bytes(part.at[pl.ds(0, (last + 1) * dp_count)], pass_send.at[kind])
+                for group in range(groups):
+                    if last > 1 and last % 2 == (group + 1) % 2:
+                        wait_bytes(text.at[pl.ds(0, 2 * (last // 2)), group], relay_send.at[group])
 
         store.wait()
         for copy in value_copies:
@@ -517,7 +519,7 @@
             dma((3,)),
             dma,
             dma((ctx_count, groups)),
-            dma,
+            dma((groups,)),
             dma((2,)),
             dma((ctx_count, 2)),
             dma((2,)),

time: 14.8 us -> 14.7 us (level)
  no operation moved by 1% of the time
where the time goes in v4:
time: 14.7 us; the launch traced here: 14.6 us
  Pallas kernels  13.9 us (95%)
  between operations  0.64 us (4%)
    pallas_call x1, Pallas kernels, fused_body(): pl.pallas_call(functools.partial(fused_kernel, sizes), out_shape=shapes,...  13.1 us
    pallas_call x1, Pallas kernels, fused_body(): pl.pallas_call(write_kernel, out_shape=shapes, in_specs=[anywhere] * 2, o...  0.83 us

profile of v4, /device:TPU:28, one launch (start us, length us, event | category | flops | bytes accessed | tf_op | source)
XLA Modules:
  0.0 14.6 jit_solution(9941992556005342086)
XLA Ops:
  0.6 13.1 %merged_attention.1 = (bf16[128,2048]{1,0:T(8,128)(2,1)S(1)}, f32[1,128]{1,0:T(1,128)S(1)}) custom-call(s32[1,8]{1,0:T(1,128)} %bitcast.13, s32[1,8]{1,0:T(1,128)} %bitcast.14, bf16[8,2,256]{2,1,0:T(2,128)(2,1)} %bitcast.11, bf16[128,256]{1,0:T(8,128)(2,1)} %bitcast.9, bf16[128,256]{1,0:T(8,128)(2,1)} %bitcast.10, bf16[16,128]{1,0:T(8,128)(2,1)} %bitcast.12, ...), custom_call_target="tpu_custom_call" | custom-call | tf_op jit(solution)/shard_map/merged_attention/pallas_call | solution.py:500
  13.7 0.8 %write_out.1 = (bf16[128,2048]{1,0:T(8,128)(2,1)}, f32[1,128]{1,0:T(1,128)}) custom-call(bf16[128,2048]{1,0:T(8,128)(2,1)S(1)} %get-tuple-element.6.attention, f32[1,128]{1,0:T(1,128)S(1)} %get-tuple-element.7.value), custom_call_target="tpu_custom_call" | custom-call | tf_op jit(solution)/shard_map/write_out/pallas_call | solution.py:535

commit v5 on v4

--- a/solution.py
+++ b/solution.py
@@ -186,13 +186,9 @@
     query_sem,
     out_sem,
     local_sem,
-    text_send,
     text_recv,
-    relay_send,
-    patch_send,
     patch_recv,
     pass_send,
-    value_send,
     value_recv,
     ready,
 ):
@@ -208,7 +204,7 @@
     partner = c + 1 - 2 * side
 
     barrier = pltpu.get_barrier_semaphore()
-    in_pair = dp_count
+    in_pair = dp_count - 1
 
     def greet(*device):
         pl.semaphore_signal(barrier, inc=1, device_id=device, device_id_type=MESH)
@@ -238,6 +234,7 @@
     def wait_bytes(ref, sem):
         copy_of(ref, ref, sem).wait()
 
+    patch_send, text_send, relay_send, value_send = local_sem, local_sem.at[2], local_sem.at[3], query_sem
     own = c * dp_count + d
     load_patches = [
         copy_of(rows_hbm, rows_in.at[own], local_sem.at[0]),
@@ -245,13 +242,13 @@
         copy_of(place_hbm, spots_in.at[own, 1], local_sem.at[1]),
     ]
     load_probe = copy_of(probe_hbm, probe_raw, local_sem.at[2])
-    load_queries = copy_of(queries_hbm, queries, query_sem)
+    load_queries = copy_of(queries_hbm, queries, query_sem.at[0])
     for load in load_patches:
         load.start()
     for group in range(groups):
         for kind, source in enumerate((keys_hbm, values_hbm)):
             copy_of(
-                source.at[:, lanes(group)], text.at[c, group, kind], text_recv.at[c, group]
+                source.at[:, lanes(group)], text.at[c, group, kind], local_sem.at[3]
             ).start()
     load_probe.start()
     load_queries.start()
@@ -267,7 +264,7 @@
     over(
         0,
         d,
-        lambda there: over(c * (1 - side), c + 1, lambda block: announce(d, there, block, t)),
+        lambda there: over(c * (1 - side), c + 1, lambda block: announce(d - 1, there, block, t)),
     )
     over(0, t, lambda other: announce(in_pair, d, c, other))
     with jax.named_scope("w_loads"):
@@ -284,7 +281,7 @@
                     src_ref=part.at[own],
                     dst_ref=part.at[own],
                     send_sem=patch_send.at[kind],
-                    recv_sem=patch_recv.at[c, kind],
+                    recv_sem=patch_recv.at[kind],
                     device_id=(there, block, t),
                     device_id_type=MESH,
                 ).start()
@@ -297,15 +294,16 @@
         over(0, d, lambda there: send_patches(there, True))
     send_patches(d, False)
     with jax.named_scope("w_text"):
-        for group in range(groups):
-            wait_bytes(text.at[c, group], text_recv.at[c, group])
+        wait_bytes(text.at[c], local_sem.at[3])
+        load_probe.wait()
+        probe[...] = probe_raw[...].astype(jnp.float32)
 
     def text_copy(group, block, there, sem):
         return pltpu.make_async_remote_copy(
             src_ref=text.at[block, group],
             dst_ref=text.at[block, group],
             send_sem=sem,
-            recv_sem=text_recv.at[block, group],
+            recv_sem=text_recv.at[group],
             device_id=(d, there, t),
             device_id_type=MESH,
         )
@@ -321,28 +319,19 @@
             def _():
                 text_copy(group, c, c + 1, text_send).start()
 
-    load_probe.wait()
-    probe[...] = probe_raw[...].astype(jnp.float32)
-
     def send_up(there):
-        pl.semaphore_wait(ready.at[there], targets + 1)
+        pl.semaphore_wait(ready.at[there - 1], targets + 1)
         send_patches(there, True)
 
-    def relay(group):
-        def hand_on(block):
-            wait_bytes(text.at[block, group], text_recv.at[block, group])
-            text_copy(group, block, partner, relay_send.at[group]).start()
-
-        @pl.when(side == (group + 1) % 2)
-        def _():
-            over(0, 2 * chip, hand_on)
+    def relay(last, group):
+        if last:
+            wait_bytes(text.at[pl.ds(0, last), group], text_recv.at[group])
+        if last % 2 == (group + 1) % 2:
+            for block in range(2 * (last // 2)):
+                text_copy(group, block, partner, relay_send).start()
 
     with jax.named_scope("up"):
         over(d + 1, dp_count, send_up)
-    with jax.named_scope("relay"):
-        for group in range(groups):
-            relay(group)
-
     def pass_patches(block):
         span = pl.ds(block * dp_count, dp_count)
         for kind, part in enumerate(parts):
@@ -350,7 +339,7 @@
                 src_ref=part.at[span],
                 dst_ref=part.at[span],
                 send_sem=pass_send.at[kind],
-                recv_sem=patch_recv.at[block, kind],
+                recv_sem=patch_recv.at[kind],
                 device_id=(d, c - 1, t),
                 device_id_type=MESH,
             ).start()
@@ -377,20 +366,20 @@
                     merged_values[group, tokens, 0:HD] = whole.astype(jnp.bfloat16)
 
     def finish(last):
+        hubs = [group for group in range(groups) if last % 2 == (group + 1) % 2]
+        others = [group for group in range(groups) if group not in hubs]
+        with jax.named_scope("relay"):
+            for group in hubs:
+                relay(last, group)
         with jax.named_scope("w_patch"):
-            for block in range(last + 1):
-                senders = dp_count if block < last else dp_count - 1
-                for kind, part in enumerate(parts):
-                    wait_bytes(
-                        part.at[pl.ds(block * dp_count, senders)], patch_recv.at[block, kind]
-                    )
-                if last % 2 and block < last - 1:
+            for kind, part in enumerate(parts):
+                wait_bytes(part.at[pl.ds(0, (last + 1) * dp_count - 1)], patch_recv.at[kind])
+            if last % 2:
+                for block in range(last - 1):
                     pass_patches(block)
         with jax.named_scope("w_kv"):
-            for group in range(groups):
-                relayed = 0 if last % 2 != (group + 1) % 2 else 2 * (last // 2)
-                for block in range(relayed, last):
-                    wait_bytes(text.at[block, group], text_recv.at[block, group])
+            for group in others:
+                relay(last, group)
             load_queries.wait()
         with jax.named_scope("attend"):
             rows = math.gcd(token_count, 16) if last % 2 and last > 1 else token_count
@@ -443,9 +432,9 @@
                 copies = chips - last // 2 - last % 2
                 if copies:
                     wait_bytes(text.at[pl.ds(0, copies)], text_send)
-                for group in range(groups):
-                    if last > 1 and last % 2 == (group + 1) % 2:
-                        wait_bytes(text.at[pl.ds(0, 2 * (last // 2)), group], relay_send.at[group])
+                relayed = 2 * (last // 2) * len([h for h in range(groups) if last % 2 == (h + 1) % 2])
+                if relayed:
+                    wait_bytes(text.at[pl.ds(0, relayed // groups)], relay_send)
 
         store.wait()
         for copy in value_copies:
@@ -514,18 +503,14 @@
             pltpu.VMEM((heads, HD), jnp.float32),
             pltpu.VMEM((1, token_count), jnp.float32),
             pltpu.VMEM((others, 1, token_count), jnp.float32),
+            dma((others,)),
             dma,
-            dma,
-            dma((3,)),
-            dma,
-            dma((ctx_count, groups)),
+            dma((4,)),
             dma((groups,)),
             dma((2,)),
-            dma((ctx_count, 2)),
             dma((2,)),
             dma((others,)),
-            dma((others,)),
-            pltpu.SemaphoreType.REGULAR((dp_count + 1,)),
+            pltpu.SemaphoreType.REGULAR((dp_count,)),
         ],
         compiler_params=pltpu.CompilerParams(
             collective_id=0, has_side_effects=True, vmem_limit_bytes=24 * 2**20
@@ -548,7 +533,7 @@
     dp_count, ctx_count, _ = sizes
     arriving = dp_count * ctx_count * patch_rows.size * patch_rows.dtype.itemsize
     arrays = (queries, keys_text, values_text, patch_rows, patch_owner, patch_place, value_head)
-    if arriving > SLOT_BYTES or ctx_count % 2:
+    if arriving > SLOT_BYTES or ctx_count % 2 or keys_text.shape[2] % (2 * HD):
         return collective_body(*arrays)
     return fused_body(sizes, *arrays)
 

time: 14.7 us -> 14.5 us (0.986)
  Pallas kernels: 13.9 us -> 13.7 us
    pallas_call x1, Pallas kernels: 13.1 us -> 12.9 us  [fused_body(): pl.pallas_call(functools.partial(fused_kernel, sizes), out_shape=shapes,...]
where the time goes in v5:
time: 14.5 us; the launch traced here: 14.4 us
  Pallas kernels  13.7 us (94%)
  between operations  0.64 us (4%)
    pallas_call x1, Pallas kernels, fused_body(): pl.pallas_call(functools.partial(fused_kernel, sizes), out_shape=shapes,...  12.9 us
    pallas_call x1, Pallas kernels, fused_body(): pl.pallas_call(write_kernel, out_shape=shapes, in_specs=[anywhere] * 2, o...  0.83 us

profile of v5, /device:TPU:28, one launch (start us, length us, event | category | flops | bytes accessed | tf_op | source)
XLA Modules:
  0.0 14.4 jit_solution(6858848404731400695)
XLA Ops:
  0.6 12.9 %merged_attention.1 = (bf16[128,2048]{1,0:T(8,128)(2,1)S(1)}, f32[1,128]{1,0:T(1,128)S(1)}) custom-call(s32[1,8]{1,0:T(1,128)} %bitcast.13, s32[1,8]{1,0:T(1,128)} %bitcast.14, bf16[8,2,256]{2,1,0:T(2,128)(2,1)} %bitcast.11, bf16[128,256]{1,0:T(8,128)(2,1)} %bitcast.9, bf16[128,256]{1,0:T(8,128)(2,1)} %bitcast.10, bf16[16,128]{1,0:T(8,128)(2,1)} %bitcast.12, ...), custom_call_target="tpu_custom_call" | custom-call | tf_op jit(solution)/shard_map/merged_attention/pallas_call | solution.py:489
  13.6 0.8 %write_out.1 = (bf16[128,2048]{1,0:T(8,128)(2,1)}, f32[1,128]{1,0:T(1,128)}) custom-call(bf16[128,2048]{1,0:T(8,128)(2,1)S(1)} %get-tuple-element.6.attention, f32[1,128]{1,0:T(1,128)S(1)} %get-tuple-element.7.value), custom_call_target="tpu_custom_call" | custom-call | tf_op jit(solution)/shard_map/write_out/pallas_call | solution.py:520

commit v6 on v5

--- a/solution.py
+++ b/solution.py
@@ -184,11 +184,9 @@
     partial,
     partial_in,
     query_sem,
-    out_sem,
     local_sem,
     text_recv,
     patch_recv,
-    pass_send,
     value_recv,
     ready,
 ):
@@ -235,6 +233,7 @@
         copy_of(ref, ref, sem).wait()
 
     patch_send, text_send, relay_send, value_send = local_sem, local_sem.at[2], local_sem.at[3], query_sem
+    pass_send, out_sem = patch_recv, text_recv.at[0]
     own = c * dp_count + d
     load_patches = [
         copy_of(rows_hbm, rows_in.at[own], local_sem.at[0]),
@@ -332,8 +331,8 @@
 
     with jax.named_scope("up"):
         over(d + 1, dp_count, send_up)
-    def pass_patches(block):
-        span = pl.ds(block * dp_count, dp_count)
+    def pass_patches(blocks):
+        span = pl.ds(0, blocks * dp_count)
         for kind, part in enumerate(parts):
             pltpu.make_async_remote_copy(
                 src_ref=part.at[span],
@@ -374,9 +373,8 @@
         with jax.named_scope("w_patch"):
             for kind, part in enumerate(parts):
                 wait_bytes(part.at[pl.ds(0, (last + 1) * dp_count - 1)], patch_recv.at[kind])
-            if last % 2:
-                for block in range(last - 1):
-                    pass_patches(block)
+            if last % 2 and last > 1:
+                pass_patches(last - 1)
         with jax.named_scope("w_kv"):
             for group in others:
                 relay(last, group)
@@ -504,10 +502,8 @@
             pltpu.VMEM((1, token_count), jnp.float32),
             pltpu.VMEM((others, 1, token_count), jnp.float32),
             dma((others,)),
-            dma,
             dma((4,)),
             dma((groups,)),
-            dma((2,)),
             dma((2,)),
             dma((others,)),
             pltpu.SemaphoreType.REGULAR((dp_count,)),
@@ -522,7 +518,7 @@
         out_shape=shapes,
         in_specs=[anywhere] * 2,
         out_specs=(pl.BlockSpec(memory_space=pltpu.HBM),) * 2,
-        scratch_shapes=[dma((math.gcd(token_count // 16, 4) + 1,))],
+        scratch_shapes=[dma((2,))],
         compiler_params=pltpu.CompilerParams(vmem_limit_bytes=2**20),
         name="write_out",
     )(*(pltpu.with_memory_space_constraint(array, pltpu.VMEM) for array in (attention, value_out)))

time: 14.5 us -> 14.5 us (level)
  no operation moved by 1% of the time
where the time goes in v6:
time: 14.5 us; the launch traced here: 14.3 us
  Pallas kernels  13.7 us (94%)
  between operations  0.64 us (4%)
    pallas_call x1, Pallas kernels, fused_body(): pl.pallas_call(functools.partial(fused_kernel, sizes), out_shape=shapes,...  12.9 us
    pallas_call x1, Pallas kernels, fused_body(): pl.pallas_call(write_kernel, out_shape=shapes, in_specs=[anywhere] * 2, o...  0.82 us

profile of v6, /device:TPU:28, one launch (start us, length us, event | category | flops | bytes accessed | tf_op | source)
XLA Modules:
  0.0 14.3 jit_solution(10824940076221282983)
XLA Ops:
  0.6 12.9 %merged_attention.1 = (bf16[128,2048]{1,0:T(8,128)(2,1)S(1)}, f32[1,128]{1,0:T(1,128)S(1)}) custom-call(s32[1,8]{1,0:T(1,128)} %bitcast.13, s32[1,8]{1,0:T(1,128)} %bitcast.14, bf16[8,2,256]{2,1,0:T(2,128)(2,1)} %bitcast.11, bf16[128,256]{1,0:T(8,128)(2,1)} %bitcast.9, bf16[128,256]{1,0:T(8,128)(2,1)} %bitcast.10, bf16[16,128]{1,0:T(8,128)(2,1)} %bitcast.12, ...), custom_call_target="tpu_custom_call" | custom-call | tf_op jit(solution)/shard_map/merged_attention/pallas_call | solution.py:487
  13.5 0.8 %write_out.1 = (bf16[128,2048]{1,0:T(8,128)(2,1)}, f32[1,128]{1,0:T(1,128)}) custom-call(bf16[128,2048]{1,0:T(8,128)(2,1)S(1)} %get-tuple-element.6.attention, f32[1,128]{1,0:T(1,128)S(1)} %get-tuple-element.7.value), custom_call_target="tpu_custom_call" | custom-call | tf_op jit(solution)/shard_map/write_out/pallas_call | solution.py:516

commit v7 on v6

--- a/solution.py
+++ b/solution.py
@@ -251,7 +251,11 @@
             ).start()
     load_probe.start()
     load_queries.start()
-    merged_values[:, :, HD:] = jnp.ones((groups, ctx_count * token_count, HD), jnp.bfloat16)
+
+    @pl.when((side == 1) & (chip > 0))
+    def _():
+        merged_values[:, :, HD:] = jnp.ones((groups, ctx_count * token_count, HD), jnp.bfloat16)
+
     with jax.named_scope("w_barrier"):
         pl.semaphore_wait(barrier, d * ctx_count + ctx_count - 1 + t)
 

time: 14.5 us -> 14.5 us (level)
  no operation moved by 1% of the time
where the time goes in v7:
time: 14.5 us; the launch traced here: 14.3 us
  Pallas kernels  13.7 us (94%)
  between operations  0.64 us (4%)
    pallas_call x1, Pallas kernels, fused_body(): pl.pallas_call(functools.partial(fused_kernel, sizes), out_shape=shapes,...  12.9 us
    pallas_call x1, Pallas kernels, fused_body(): pl.pallas_call(write_kernel, out_shape=shapes, in_specs=[anywhere] * 2, o...  0.82 us

profile of v7, /device:TPU:28, one launch (start us, length us, event | category | flops | bytes accessed | tf_op | source)
XLA Modules:
  0.0 14.3 jit_solution(13581065879187690646)
XLA Ops:
  0.6 12.9 %merged_attention.1 = (bf16[128,2048]{1,0:T(8,128)(2,1)S(1)}, f32[1,128]{1,0:T(1,128)S(1)}) custom-call(s32[1,8]{1,0:T(1,128)} %bitcast.13, s32[1,8]{1,0:T(1,128)} %bitcast.14, bf16[8,2,256]{2,1,0:T(2,128)(2,1)} %bitcast.11, bf16[128,256]{1,0:T(8,128)(2,1)} %bitcast.9, bf16[128,256]{1,0:T(8,128)(2,1)} %bitcast.10, bf16[16,128]{1,0:T(8,128)(2,1)} %bitcast.12, ...), custom_call_target="tpu_custom_call" | custom-call | tf_op jit(solution)/shard_map/merged_attention/pallas_call | solution.py:491
  13.5 0.8 %write_out.1 = (bf16[128,2048]{1,0:T(8,128)(2,1)}, f32[1,128]{1,0:T(1,128)}) custom-call(bf16[128,2048]{1,0:T(8,128)(2,1)S(1)} %get-tuple-element.6.attention, f32[1,128]{1,0:T(1,128)S(1)} %get-tuple-element.7.value), custom_call_target="tpu_custom_call" | custom-call | tf_op jit(solution)/shard_map/write_out/pallas_call | solution.py:520
